TPU v7x, 32 devices: a whole 2x2x4 slice. The times are simulated.
32 devices in a mesh: dp: 2 (over x), ffn: 4 (over z), emb: 4 (over y, core).
Axes of the slice: x: 2, y: 2, z: 4, core: 2. Of those that a mesh axis runs over, the one named last changes fastest.
Arguments:
- hidden: bfloat16 [256, 2048], P('dp', 'emb'), parts along dimension 0
- norm_pre: bfloat16 [2048], P('emb')
- norm_post: bfloat16 [2048], P('emb')
- w_router: bfloat16 [2048, 128], P('emb')
- w_gate: bfloat16 [128, 2048, 768], P(None, 'emb', 'ffn')
- w_up: bfloat16 [128, 2048, 768], P(None, 'emb', 'ffn')
- w_down: bfloat16 [128, 768, 2048], P(None, 'ffn', 'emb')
- choice: int32 [256, 8], P('dp'), parts along dimension 0
Outputs:
- output: bfloat16 [256, 2048], P('dp', 'emb'), parts along dimension 0
There are 2 independent parts. A program takes and returns all parts, laid end to end along the dimension named above; an argument that names none is the same for every part.
All inputs are finite; a program needn't handle non-finite values.
Results may differ from a plain program's by a relative error of at most 0.0119329.
Values are sent between devices in bfloat16 or wider.
A program may use at most 1 GiB of HBM per device.

v0:
```python
import jax
import jax.numpy as jnp
from jax import lax
from jax.sharding import PartitionSpec as P

EPS = 1e-5


def route_tokens(choice, router_prob, experts, capacity):
    num_tok, top_k = choice.shape
    onehot = (choice[:, :, None] == jnp.arange(experts)[None, None, :]).astype(jnp.int32)
    assigned = jnp.sum(onehot, axis=1)
    before = jnp.cumsum(assigned, axis=0) - assigned
    slot_idx = jnp.sum(onehot * before[:, None, :], axis=2)
    position = jnp.where(slot_idx < capacity, choice * capacity + slot_idx, experts * capacity)
    gate_val = jnp.take_along_axis(router_prob, choice, axis=1)
    flat_pos = position.reshape(-1)
    token_ids = jnp.repeat(jnp.arange(num_tok, dtype=jnp.int32), top_k)
    slot_token = jnp.full((experts * capacity,), num_tok, jnp.int32).at[flat_pos].set(token_ids, mode='drop')
    slot_gate = jnp.zeros((experts * capacity,), jnp.float32).at[flat_pos].set(gate_val.reshape(-1), mode='drop')
    return position, slot_token, slot_gate


def solution(mesh):
    emb_size = mesh.shape['emb']

    def local_block(hidden, norm_pre, norm_post, w_router, w_gate, w_up, w_down, choice):
        num_tok, local_width = hidden.shape
        model_width = local_width * emb_size
        experts = w_gate.shape[0]
        top_k = choice.shape[1]
        capacity = 2 * num_tok * top_k // experts
        hid_f32 = hidden.astype(jnp.float32)
        sq_pre = lax.psum(jnp.sum(hid_f32 * hid_f32, axis=1, keepdims=True), 'emb')
        inv_pre = lax.rsqrt(sq_pre / model_width + EPS)
        normed = (hid_f32 * inv_pre * norm_pre.astype(jnp.float32)).astype(jnp.bfloat16)
        logits = lax.psum(jnp.dot(normed, w_router, preferred_element_type=jnp.float32), 'emb')
        router_prob = jax.nn.softmax(logits, axis=1)
        position, slot_token, slot_gate = route_tokens(choice, router_prob, experts, capacity)
        expert_in = jnp.take(normed, slot_token, axis=0, mode='fill', fill_value=0).reshape(experts, capacity, local_width)
        z_gate = jnp.einsum('ecd,edf->ecf', expert_in, w_gate, preferred_element_type=jnp.float32).astype(jnp.bfloat16)
        z_up = jnp.einsum('ecd,edf->ecf', expert_in, w_up, preferred_element_type=jnp.float32).astype(jnp.bfloat16)
        z_gate, z_up = lax.psum((z_gate, z_up), 'emb')
        act_val = (jax.nn.gelu(z_gate.astype(jnp.float32), approximate=True) * z_up.astype(jnp.float32)).astype(jnp.bfloat16)
        part_out = jnp.einsum('ecf,efd->ecd', act_val, w_down, preferred_element_type=jnp.float32).astype(jnp.bfloat16)
        expert_out = lax.psum(part_out, 'ffn')
        weighted = (expert_out.reshape(experts * capacity, local_width).astype(jnp.float32) * slot_gate[:, None]).astype(jnp.bfloat16)
        picked = jnp.take(weighted, position, axis=0, mode='fill', fill_value=0)
        mix_sum = jnp.sum(picked.astype(jnp.float32), axis=1)
        sq_post = lax.psum(jnp.sum(mix_sum * mix_sum, axis=1, keepdims=True), 'emb')
        inv_post = lax.rsqrt(sq_post / model_width + EPS)
        return (hid_f32 + mix_sum * inv_post * norm_post.astype(jnp.float32)).astype(jnp.bfloat16)

    in_specs = (P('dp', 'emb'), P('emb'), P('emb'), P('emb', None), P(None, 'emb', 'ffn'), P(None, 'emb', 'ffn'), P(None, 'ffn', 'emb'), P('dp', None))
    return jax.shard_map(local_block, mesh=mesh, in_specs=in_specs, out_specs=P('dp', 'emb'), check_vma=False)
```

profile of v0, /device:TPU:0, one launch (start us, length us, event | category | flops | bytes accessed | tf_op | source)
XLA Modules:
  0.0 253.3 jit_solution(12764003977280493731)
XLA Ops:
  6.5 0.8 copy.27
  7.4 0.2 convert_reduce_fusion.1
  7.6 0.2 reduce_window_sum.11
  7.8 2.4 select_reduce_fusion
  10.2 0.7 compare_and_fusion.1
  11.3 4.3 %scatter_custom_fusion = s32[2048]{0:T(1024)S(1)} fusion(s32[1024]{0:T(1024)S(1)} %bitcast.27, s32[1024]{0:T(1024)S(1)} %reshape.112, s32[]{:T(128)} %constant.34.clone.1), kind=kCustom, calls=%fused_computation.54 | custom fusion | bytes 8196 | tf_op jit(solution)/shard_map/scatter | solution.py:19
  15.6 1.0 fusion.18
  16.6 8.4 %psum.42 = f32[128,1]{0,1:T(1,128)S(1)} all-reduce(f32[128,1]{0,1:T(1,128)S(1)} %bitcast.29), channel_id=1, replica_groups=mesh['dp'=2,'ffn'=4,'emb'=4] {'emb'}, use_global_device_ids=true, to_apply=%region_5.0 | all-reduce | flops 128 | bytes 1024 | tf_op jit(solution)/shard_map/psum | solution.py:34
  25.1 0.7 convert_element_type.50
  25.9 1.0 fusion.20
  26.9 7.5 %gather_fusion = bf16[2048,512]{1,0:T(8,128)(2,1)S(1)} fusion(bf16[128,512]{1,0:T(8,128)(2,1)S(1)} %fusion.20, s32[2048]{0:T(1024)S(1)} %fusion.24), kind=kCustom, calls=%fused_computation | custom fusion | bytes 4202496 | tf_op jit(solution)/shard_map/jit(_take)/gather | solution.py:40
  34.4 12.7 %fusion.10 = bf16[128,16,192]{2,1,0:T(8,128)(2,1)} fusion(bf16[128,512,192]{1,2,0:T(8,128)(2,1)} %param.13, bf16[128,16,512]{2,1,0:T(8,128)(2,1)S(1)} %bitcast.24, pred[128,16]{1,0:T(8,128)(4,1)S(1)} %broadcast_in_dim.63), kind=kOutput, calls=%fused_computation.23 | convolution fusion | flops 404094976 | bytes 28051456 | tf_op jit(solution)/shard_map/ecd,edf->ecf/dot_general | solution.py:42
  47.1 12.6 %fusion.9 = bf16[128,16,192]{2,1,0:T(8,128)(2,1)} fusion(bf16[128,512,192]{1,2,0:T(8,128)(2,1)} %param.12, bf16[128,16,512]{2,1,0:T(8,128)(2,1)S(1)} %bitcast.25, pred[128,16]{1,0:T(8,128)(4,1)S(1)} %broadcast_in_dim.63), kind=kOutput, calls=%fused_computation.22 | convolution fusion | flops 404094976 | bytes 28051456 | tf_op jit(solution)/shard_map/ecd,edf->ecf/dot_general | solution.py:41
  59.8 0.8 fusion.35
  60.6 0.2 all-reduce.5.cloned.1.call-start
  60.8 50.6 %all-reduce.9.cloned.1.call-done = (bf16[128,16,192]{2,1,0:T(8,128)(2,1)}, bf16[128,16,192]{2,1,0:T(8,128)(2,1)}) async-done(((bf16[128,16,192]{2,1,0:T(8,128)(2,1)}, bf16[128,16,192]{2,1,0:T(8,128)(2,1)}), (bf16[128,16,192]{2,1,0:T(8,128)(2,1)}, bf16[128,16,192]{2,1,0:T(8,128)(2,1)})) %all-reduce.9.cloned.1.call-update) | async-done | bytes 1572880 | tf_op jit(solution)/shard_map/psum | solution.py:43
  111.4 13.6 %convolution_convert_fusion = bf16[128,16,512]{2,1,0:T(8,128)(2,1)} fusion(bf16[128,192,512]{2,1,0:T(8,128)(2,1)} %param.14, bf16[128,16,192]{2,1,0:T(8,128)(2,1)} %get-tuple-element.5, bf16[128,16,192]{2,1,0:T(8,128)(2,1)} %get-tuple-element.6), kind=kOutput, calls=%fused_computation.19 | convolution fusion | flops 408420352 | bytes 28835840 | tf_op jit(solution)/shard_map/ecf,efd->ecd/dot_general | solution.py:45
  125.0 0.7 copy-done.4
  125.9 0.1 copy.30
  126.3 19.0 %all-reduce.7.cloned.1.call-done = f32[128,128]{1,0:T(8,128)} async-done(((f32[128,128]{1,0:T(8,128)}), f32[128,128]{1,0:T(8,128)}) %all-reduce.7.cloned.1.call-update) | async-done | bytes 65552 | tf_op jit(solution)/shard_map/psum | solution.py:37
  145.3 0.9 reduce_max.9
  146.2 1.0 fusion.23
  147.3 1.0 fusion.22
  148.2 6.8 %gather_fusion.2 = f32[1024]{0:T(1024)S(1)} fusion(f32[128,128]{1,0:T(8,128)S(1)} %fusion.22, s32[1024]{0:T(1024)S(1)} %reshape.102), kind=kCustom, calls=%fused_computation.2 | custom fusion | bytes 16384 | tf_op jit(solution)/shard_map/jit(take_along_axis)/gather | solution.py:16
  155.2 0.1 copy.34
  155.4 4.3 %scatter_custom_fusion.1 = f32[2048]{0:T(1024)S(1)} fusion(s32[1024]{0:T(1024)S(1)} %bitcast.28, f32[1024]{0:T(1024)S(1)} %reshape.120, f32[]{:T(128)} %constant.42.clone.1), kind=kCustom, calls=%fused_computation.52 | custom fusion | bytes 8196 | tf_op jit(solution)/shard_map/scatter | solution.py:20
  159.7 73.6 %all-reduce.5.cloned.1.call-done = bf16[2048,512]{1,0:T(8,128)(2,1)} async-done(((bf16[2048,512]{1,0:T(8,128)(2,1)}), bf16[2048,512]{1,0:T(8,128)(2,1)}) %all-reduce.5.cloned.1.call-update) | async-done | bytes 2097168 | tf_op jit(solution)/shard_map/psum | solution.py:46
  233.3 2.0 multiply_convert_fusion
  235.4 4.0 %gather_fusion.1 = bf16[1024,512]{1,0:T(8,128)(2,1)S(1)} fusion(bf16[2048,512]{1,0:T(8,128)(2,1)S(1)} %multiply_convert_fusion, s32[1024]{0:T(1024)S(1)} %broadcast_clamp_fusion), kind=kCustom, calls=%fused_computation.1 | custom fusion | bytes 2101248 | tf_op jit(solution)/shard_map/jit(_take)/gather | solution.py:48
  239.4 0.7 convert_reduce_fusion
  240.2 5.8 %psum.47 = f32[128,1]{0,1:T(1,128)S(1)} all-reduce(f32[128,1]{0,1:T(1,128)S(1)} %bitcast.30), channel_id=1, replica_groups=mesh['dp'=2,'ffn'=4,'emb'=4] {'emb'}, use_global_device_ids=true, to_apply=%region_15.16 | all-reduce | flops 128 | bytes 1024 | tf_op jit(solution)/shard_map/psum | solution.py:50
  246.0 0.8 fusion.21
  (39 shorter events, 1.4 us)
Async XLA Ops:
  6.5 53.2 %copy-start = (bf16[512,128]{1,0:T(8,128)(2,1)S(1)}, bf16[512,128]{1,0:T(8,128)(2,1)}, u32[]{:S(2)}) copy-start(bf16[512,128]{1,0:T(8,128)(2,1)} %param.11) | copy-start | bytes 393220
  6.5 104.9 %all-reduce.9.cloned.1.call-start = ((), (), s32[]{:S(2)}) async-start(), calls=%async_computation.2 | async-start | bytes 4194304 | tf_op jit(solution)/shard_map/psum | solution.py:43
  59.7 85.6 %all-reduce.7.cloned.1.call-start = ((), (), s32[]{:S(2)}) async-start(), calls=%async_computation.1 | async-start | bytes 131072 | tf_op jit(solution)/shard_map/psum | solution.py:37
  60.6 172.7 %all-reduce.5.cloned.1.call-start = ((), (), s32[]{:S(2)}) async-start(), calls=%async_computation | async-start | bytes 4194304 | tf_op jit(solution)/shard_map/psum | solution.py:46
  125.0 0.7 copy-start.4
  125.0 0.7 copy-start.3
  235.4 10.7 %copy-start.2 = (bf16[128,512]{1,0:T(8,128)(2,1)S(1)}, bf16[128,512]{1,0:T(8,128)(2,1)}, u32[]{:S(2)}) copy-start(bf16[128,512]{1,0:T(8,128)(2,1)} %param.8) | copy-start | bytes 393220
  235.4 11.4 %copy-start.1 = (bf16[512,128]{1,0:T(8,128)(2,1)S(1)}, bf16[512,128]{1,0:T(8,128)(2,1)}, u32[]{:S(2)}) copy-start(bf16[512,128]{1,0:T(8,128)(2,1)} %param.11) | copy-start | bytes 393220
Sparse Core Ops, SparseCore 0:
  59.8 51.5 all-reduce.8
  113.7 31.5 all-reduce.6
  147.7 85.6 all-reduce.4
where the time goes:
time: 254 us; the launch traced here: 253 us
  waiting for transfers between devices  143 us (56%)
  matrix products  39.7 us (16%)
  local copies, waits for them, and re-layouts  29.7 us (12%)
  blocking collectives  14.3 us (6%)
  between operations  13.3 us (5%)
  other arithmetic  12.8 us (5%)
    psum x1, waiting for transfers between devices, local_block(): expert_out = lax.psum(part_out, 'ffn')  73.6 us
    psum x1, waiting for transfers between devices, local_block(): z_gate, z_up = lax.psum((z_gate, z_up), 'emb')  50.6 us
    psum x1, waiting for transfers between devices, local_block(): lax.psum(jnp.dot(normed, w_router, preferred_element_type=jnp.float32), '...  19 us
    dot_general x1, matrix products, local_block(): jnp.einsum('ecf,efd->ecd', act_val, w_down, preferred_element_type=jnp.fl...  13.6 us
    dot_general x1, matrix products, local_block(): jnp.einsum('ecd,edf->ecf', expert_in, w_up, preferred_element_type=jnp.fl...  12.7 us
    dot_general x1, matrix products, local_block(): jnp.einsum('ecd,edf->ecf', expert_in, w_gate, preferred_element_type=jnp....  12.6 us
    psum x1, blocking collectives, local_block(): sq_pre = lax.psum(jnp.sum(hid_f32 * hid_f32, axis=1, keepdims=True), 'emb')  8.44 us
    gather x1, local copies, waits for them, and re-layouts, local_block(): jnp.take(normed, slot_token, axis=0, mode='fill', fill_value=0)  7.54 us
  transfers between devices with their start and end apart: 3, of which 3 were waited for; matrix products, arithmetic and copies ran while one was open for 12% of the time, Pallas kernels for 0%

commit v1 on v0

v1 whole, which is shorter than its diff:
```python
import functools

import jax
import jax.numpy as jnp
from jax import lax
from jax.experimental import pallas as pl
from jax.experimental.pallas import tpu as pltpu
from jax.sharding import PartitionSpec as P

EPS = 1e-5
MESH = pl.DeviceIdType.MESH
BF = jnp.bfloat16
F32 = jnp.float32
RING = 6
EB = 8
CAP = 16
NB = 16


def remote(src, dst, send, recv, **where):
    return pltpu.make_async_remote_copy(
        src_ref=src, dst_ref=dst, send_sem=send, recv_sem=recv,
        device_id=where, device_id_type=MESH)


def kernel(model_width, h_ref, pre_ref, post_ref, wr_ref, choice_ref, w0_ref, w1_ref, w2_ref, o_ref,
           ring, w2buf, oht, oh, bnorm, zsend, recv1, snd2, recv2, own2, gall, pos_ref, pt_ref,
           lbuf, lrecv1, lsnd2, lrecv2, pbuf, sq_snd, sq_recv, macc, ubuf, mrecv, mown, tq_snd, tq_recv, obuf,
           ring_sem, w2_sem, s1_s, s1_r, s2_s, s2_r, gy_s, gy_r, gp_s, gp_r, gf_s, gf_r,
           l_s, l_r, sq_s, sq_r, rs_s, rs_r, tq_s, tq_r, ag_s, ag_r):
    ffn = lax.axis_index("ffn")
    emb = lax.axis_index("emb")
    core = emb % 2
    row = emb // 2
    partner = emb + 1 - 2 * core
    across = (emb + 2) % 4
    tok = h_ref.shape[0]
    half = EB * CAP // 2
    quarter = half // 2
    ROWS = EB * CAP

    def ring_copies(batch):
        slot = batch % RING
        e0 = pl.ds(batch * EB, EB)
        return [
            pltpu.make_async_copy(w0_ref.at[e0, pl.ds(0, 128)], ring.at[slot, :, pl.ds(0, 128)], ring_sem.at[slot, 0]),
            pltpu.make_async_copy(w1_ref.at[e0, pl.ds(0, 128)], ring.at[slot, :, pl.ds(128, 128)], ring_sem.at[slot, 1]),
            pltpu.make_async_copy(w0_ref.at[e0, pl.ds(128, 64)], ring.at[slot, :, pl.ds(256, 64)], ring_sem.at[slot, 2]),
            pltpu.make_async_copy(w1_ref.at[e0, pl.ds(128, 64)], ring.at[slot, :, pl.ds(320, 64)], ring_sem.at[slot, 3]),
        ]

    def w2_copy(batch):
        e0 = pl.ds(batch * EB, EB)
        return pltpu.make_async_copy(w2_ref.at[e0], w2buf.at[e0], w2_sem.at[batch])

    for b in range(RING):
        for c in ring_copies(b):
            c.start()

    hf = h_ref[...].astype(F32)
    sq = jnp.sum(hf * hf, axis=1, keepdims=True)
    sq_rows = jnp.transpose(jnp.broadcast_to(sq, (tok, tok)))
    sq_snd[...] = sq_rows[0:8]

    barrier = pltpu.get_barrier_semaphore()
    for d in range(1, 4):
        pl.semaphore_signal(barrier, inc=1, device_id={"emb": (emb + d) % 4}, device_id_type=MESH)
        pl.semaphore_signal(barrier, inc=1, device_id={"ffn": (ffn + d) % 4}, device_id_type=MESH)
    pl.semaphore_wait(barrier, 6)

    def sq_copy(d):
        return remote(sq_snd, sq_recv.at[d - 1], sq_s.at[d - 1], sq_r.at[d - 1], emb=(emb + d) % 4)

    for d in range(1, 4):
        sq_copy(d).start()

    experts = lax.broadcasted_iota(jnp.int32, (tok, tok), 0)
    lanes = lax.broadcasted_iota(jnp.int32, (tok, tok), 1)
    assigned = jnp.zeros((tok, tok), F32)
    for k in range(choice_ref.shape[0]):
        assigned = assigned + (jnp.broadcast_to(choice_ref[k:k + 1, :], (tok, tok)) == experts).astype(F32)
    upper = (experts < lanes).astype(F32).astype(BF)
    before = jnp.dot(assigned.astype(BF), upper, preferred_element_type=F32)
    pos_ref[...] = jnp.where(assigned > 0.5, before, 1000.0)
    slot_no = lax.broadcasted_iota(jnp.int32, (CAP, tok), 0).astype(F32)

    def build(b, carry):
        rows = pos_ref[pl.ds(pl.multiple_of(b * EB, EB), EB), :]
        hot = jnp.concatenate(
            [(jnp.broadcast_to(rows[e:e + 1, :], (CAP, tok)) == slot_no).astype(F32) for e in range(EB)], axis=0)
        oht[b] = hot.astype(BF)
        oh[b] = jnp.transpose(hot).astype(BF)
        return carry

    lax.fori_loop(0, NB, build, 0)

    total = sq_snd[...]
    for d in range(1, 4):
        sq_copy(d).wait_recv()
    for d in range(1, 4):
        total = total + sq_recv[d - 1]
    inv_rows = lax.rsqrt(total / model_width + EPS)
    inv = jnp.transpose(jnp.broadcast_to(inv_rows[0:1, :], (tok, tok)))[:, 0:1]
    bnorm[...] = (h_ref[...].astype(F32) * inv * pre_ref[...].astype(F32)).astype(BF)

    lbuf[...] = jnp.dot(bnorm[...], wr_ref[...], preferred_element_type=F32)
    htok = tok // 2
    mine = pl.ds(pl.multiple_of(core * htok, htok), htok)

    def logit_pair():
        return remote(lbuf, lrecv1, l_s.at[0], l_r.at[0], emb=partner)

    def logit_across():
        return remote(lsnd2, lrecv2, l_s.at[1], l_r.at[1], emb=across)

    def prob_pair():
        return remote(pbuf.at[mine], pbuf.at[mine], l_s.at[2], l_r.at[2], emb=partner)

    logit_pair().start()

    def z_pair(j):
        return remote(zsend.at[j, pl.ds(pl.multiple_of((1 - core) * half, half), half)], recv1.at[j],
                      s1_s.at[j], s1_r.at[j], emb=partner)

    def z_across(j):
        return remote(snd2.at[j], recv2.at[j], s2_s.at[j], s2_r.at[j], emb=across)

    own_rows = pl.ds(pl.multiple_of(core * half + row * quarter, quarter), quarter)
    other_rows = pl.ds(pl.multiple_of(core * half + (1 - row) * quarter, quarter), quarter)

    def g_across(k):
        return remote(gall.at[k, own_rows], gall.at[k, own_rows], gy_s.at[k], gy_r.at[k], emb=across)

    def g_pair(k):
        return remote(gall.at[k, own_rows], gall.at[k, own_rows], gp_s.at[k], gp_r.at[k], emb=partner)

    def g_forward(k):
        return remote(gall.at[k, other_rows], gall.at[k, other_rows], gf_s.at[k], gf_r.at[k], emb=partner)

    macc[...] = jnp.zeros_like(macc)

    def step(i, carry):
        @pl.when(i < NB)
        def _():
            slot = i % RING
            for c in ring_copies(i):
                c.wait()
            x = jnp.dot(oht[i], bnorm[...], preferred_element_type=F32).astype(BF)
            for e in range(EB):
                z = lax.dot_general(x[e * CAP:(e + 1) * CAP], ring[slot, e], (((1,), (1,)), ((), ())),
                                    preferred_element_type=F32)
                zsend[i, e * CAP:(e + 1) * CAP, :] = z.astype(BF)
            z_pair(i).start()

            @pl.when(i + RING < NB)
            def _():
                for c in ring_copies(i + RING):
                    c.start()
            w2_copy(i).start()

        @pl.when((i >= 1) & (i < NB + 1))
        def _():
            j = i - 1
            z_pair(j).wait_recv()
            snd2[j] = (zsend[j, other_rows, :].astype(F32)
                       + recv1[j, pl.ds(pl.multiple_of((1 - row) * quarter, quarter), quarter), :].astype(F32)).astype(BF)
            z_across(j).start()
            own2[j] = (zsend[j, own_rows, :].astype(F32)
                       + recv1[j, pl.ds(pl.multiple_of(row * quarter, quarter), quarter), :].astype(F32))

        @pl.when((i >= 3) & (i < NB + 3))
        def _():
            k = i - 3
            z_across(k).wait_recv()
            z = (own2[k] + recv2[k].astype(F32)).astype(BF).astype(F32)
            low = jax.nn.gelu(z[:, 0:128], approximate=True) * z[:, 128:256]
            mixed = z[:, 256:384]
            high = jax.nn.gelu(mixed, approximate=True) * pltpu.roll(mixed, 64, 1)
            gall[k, own_rows, 0:128] = low.astype(BF)
            gall[k, own_rows, 128:256] = high.astype(BF)
            g_across(k).start()
            g_pair(k).start()

        @pl.when((i >= 5) & (i < NB + 5))
        def _():
            g_across(i - 5).wait_recv()
            g_forward(i - 5).start()

        @pl.when(i == 2)
        def _():
            logit_pair().wait_recv()
            lbuf2 = lbuf[mine, :] + lrecv1[mine, :]
            lsnd2[...] = lbuf2
            logit_across().start()

        @pl.when(i == 5)
        def _():
            logit_across().wait_recv()
            logits = lsnd2[...] + lrecv2[...]
            pbuf[mine, :] = jax.nn.softmax(logits, axis=1)
            prob_pair().start()

        @pl.when(i == 8)
        def _():
            prob_pair().wait_recv()
            pt_ref[...] = jnp.transpose(pbuf[...])

        @pl.when(i >= NB)
        def _():
            b = i - NB
            w2_copy(b).wait()
            g_pair(b).wait_recv()
            g_forward(b).wait_recv()
            probs = pt_ref[pl.ds(pl.multiple_of(b * EB, EB), EB), :]
            for e in range(EB):
                rows = slice(e * CAP, (e + 1) * CAP)
                y = jnp.dot(gall[b, rows, 0:192], w2buf[b * EB + e], preferred_element_type=F32)
                gate = jnp.sum(oht[b, rows, :].astype(F32) * probs[e:e + 1, :], axis=1, keepdims=True)
                ubuf[rows, :] = (y.astype(BF).astype(F32) * gate).astype(BF)
            macc[...] += jnp.dot(oh[b], ubuf[...], preferred_element_type=F32)
        return carry

    lax.fori_loop(0, 2 * NB, step, 0)

    part = tok // 4

    def rs_copy(d):
        peer = (ffn + d) % 4
        return remote(macc.at[pl.ds(pl.multiple_of(peer * part, part), part)], mrecv.at[d - 1],
                      rs_s.at[d - 1], rs_r.at[d - 1], ffn=peer)

    for d in (2, 1, 3):
        rs_copy(d).start()
    my_tok = pl.ds(pl.multiple_of(ffn * part, part), part)
    m = macc[my_tok, :]

    def drain(j, carry):
        z_pair(j).wait_send()
        z_across(j).wait_send()
        g_across(j).wait_send()
        g_pair(j).wait_send()
        g_forward(j).wait_send()
        return carry

    lax.fori_loop(0, NB, drain, 0)
    logit_pair().wait_send()
    logit_across().wait_send()
    prob_pair().wait_send()
    for d in range(1, 4):
        sq_copy(d).wait_send()
        rs_copy(d).wait_recv()
    for d in range(1, 4):
        m = m + mrecv[d - 1]
    mown[...] = m
    m2 = m * m
    tq_snd[...] = m2[:, 0:128] + m2[:, 128:256] + m2[:, 256:384] + m2[:, 384:512]

    def tq_copy(d):
        return remote(tq_snd, tq_recv.at[d - 1], tq_s.at[d - 1], tq_r.at[d - 1], emb=(emb + d) % 4)

    for d in range(1, 4):
        tq_copy(d).start()
    for d in range(1, 4):
        rs_copy(d).wait_send()
        tq_copy(d).wait_recv()
    tot = tq_snd[...]
    for d in range(1, 4):
        tot = tot + tq_recv[d - 1]
    inv_post = lax.rsqrt(jnp.sum(tot, axis=1, keepdims=True) / model_width + EPS)
    res = h_ref[my_tok, :].astype(F32) + mown[...] * inv_post * post_ref[...].astype(F32)
    obuf[my_tok, :] = res.astype(BF)

    def ag_copy(d):
        return remote(obuf.at[my_tok], obuf.at[my_tok], ag_s.at[d - 1], ag_r.at[d - 1], ffn=(ffn + d) % 4)

    for d in (2, 1, 3):
        ag_copy(d).start()
    for d in range(1, 4):
        tq_copy(d).wait_send()
        ag_copy(d).wait_recv()
    o_ref[...] = obuf[...]
    for d in range(1, 4):
        ag_copy(d).wait_send()


def solution(mesh):
    emb_size = mesh.shape['emb']

    def local_block(hidden, norm_pre, norm_post, w_router, w_gate, w_up, w_down, choice):
        tok, width = hidden.shape
        experts, _, fw = w_gate.shape
        dma = pltpu.SemaphoreType.DMA
        vm = pltpu.VMEM
        rows = EB * CAP
        vspec = pl.BlockSpec(memory_space=pltpu.VMEM)
        hspec = pl.BlockSpec(memory_space=pl.ANY)
        return pl.pallas_call(
            functools.partial(kernel, width * emb_size),
            out_shape=jax.ShapeDtypeStruct((tok, width), BF),
            in_specs=[vspec] * 5 + [hspec] * 3,
            out_specs=vspec,
            scratch_shapes=[
                vm((RING, EB, 2 * fw, width), BF), vm((experts, fw, width), BF),
                vm((NB, rows, tok), BF), vm((NB, tok, rows), BF), vm((tok, width), BF),
                vm((NB, rows, 2 * fw), BF), vm((NB, rows // 2, 2 * fw), BF),
                vm((NB, rows // 4, 2 * fw), BF), vm((NB, rows // 4, 2 * fw), BF), vm((NB, rows // 4, 2 * fw), F32),
                vm((NB, rows, 256), BF), vm((experts, tok), F32), vm((experts, tok), F32),
                vm((tok, experts), F32), vm((tok, experts), F32), vm((tok // 2, experts), F32),
                vm((tok // 2, experts), F32), vm((tok, experts), F32),
                vm((8, tok), F32), vm((3, 8, tok), F32),
                vm((tok, width), F32), vm((rows, width), BF), vm((3, tok // 4, width), F32), vm((tok // 4, width), F32),
                vm((tok // 4, 128), F32), vm((3, tok // 4, 128), F32), vm((tok, width), BF),
                dma((RING, 4)), dma((NB,)),
                dma((NB,)), dma((NB,)), dma((NB,)), dma((NB,)), dma((NB,)), dma((NB,)),
                dma((NB,)), dma((NB,)), dma((NB,)), dma((NB,)),
                dma((3,)), dma((3,)), dma((3,)), dma((3,)), dma((3,)), dma((3,)), dma((3,)), dma((3,)), dma((3,)), dma((3,)),
            ],
            compiler_params=pltpu.CompilerParams(
                collective_id=0, has_side_effects=True, vmem_limit_bytes=67043328),
        )(hidden, norm_pre.reshape(1, width), norm_post.reshape(1, width), w_router, choice.T,
          jnp.swapaxes(w_gate, 1, 2), jnp.swapaxes(w_up, 1, 2), w_down)

    in_specs = (P('dp', 'emb'), P('emb'), P('emb'), P('emb', None), P(None, 'emb', 'ffn'), P(None, 'emb', 'ffn'), P(None, 'ffn', 'emb'), P('dp', None))
    return jax.shard_map(local_block, mesh=mesh, in_specs=in_specs, out_specs=P('dp', 'emb'), check_vma=False)
```

time: 254 us -> 65.4 us (0.26)
  waiting for transfers between devices: 143 us -> 0 us
  Pallas kernels: 0 us -> 61.1 us
  matrix products: 39.7 us -> 0 us
  local copies, waits for them, and re-layouts: 29.7 us -> 4.09 us
  blocking collectives: 14.3 us -> 0 us
  between operations: 13.3 us -> 0.01 us
  other arithmetic: 12.8 us -> 0 us
    psum x3 -> x0, waiting for transfers between devices: 143 us -> none  [the longest x1 73.6 us: local_block(): expert_out = lax.psum(part_out, 'ffn')]
    pallas_call x0 -> x1, Pallas kernels: none -> 61.1 us  [local_block(): pl.pallas_call(functools.partial(kernel, width * emb_size), out_shape=jax...]
    dot_general x4 -> x0, matrix products: 39.7 us -> none  [the longest x1 13.6 us: local_block(): jnp.einsum('ecf,efd->ecd', act_val, w_down, preferred_element_type=jnp.fl...]
    gather x7 -> x0, local copies, waits for them, and re-layouts: 18.6 us -> none  [the longest x1 7.54 us: local_block(): jnp.take(normed, slot_token, axis=0, mode='fill', fill_value=0)]
    psum x2 -> x0, blocking collectives: 14.3 us -> none  [the longest x1 8.44 us: local_block(): sq_pre = lax.psum(jnp.sum(hid_f32 * hid_f32, axis=1, keepdims=True), 'emb')]
    scatter x2 -> x0, local copies, waits for them, and re-layouts: 8.63 us -> none  [the longest x1 4.32 us: route_tokens(): jnp.full((experts * capacity,), num_tok, jnp.int32).at[flat_pos]]
    reduce_sum x6 -> x0, other arithmetic: 5.46 us -> none  [the longest x1 2.39 us: route_tokens(): slot_idx = jnp.sum(onehot * before[:, None, :], axis=2)]
    convert_element_type x5 -> x0, other arithmetic: 4.5 us -> none  [the longest x1 2.04 us: local_block(): (expert_out.reshape(experts * capacity, local_width).astype(jnp.float32)...]
  transfers between devices with their start and end apart: 3 -> 0, of which waited for: 3 -> 0; matrix products, arithmetic and copies ran while one was open for 12% -> 0% of each run, Pallas kernels for 0% -> 0%
where the time goes in v1:
time: 65.4 us; the launch traced here: 65.2 us
  Pallas kernels  61.1 us (93%)
  local copies, waits for them, and re-layouts  4.09 us (6%)
    pallas_call x1, Pallas kernels, local_block(): pl.pallas_call(functools.partial(kernel, width * emb_size), out_shape=jax...  61.1 us
    unnamed x1, local copies, waits for them, and re-layouts  1.57 us

profile of v1, /device:TPU:0, one launch (start us, length us, event | category | flops | bytes accessed | tf_op | source)
XLA Modules:
  0.0 65.2 jit_solution(10582989622385327552)
XLA Ops:
  0.0 1.3 %reshape.6.pre_ref = bf16[1,512]{1,0:T(2,128)(2,1)} reshape(bf16[512]{0:T(512)(128)(2,1)} %param.9) | data formatting | bytes 2048 | tf_op jit(solution)/shard_map/reshape | solution.py:320
  1.3 1.3 %reshape.7.post_ref = bf16[1,512]{1,0:T(2,128)(2,1)} reshape(bf16[512]{0:T(512)(128)(2,1)} %param.10) | data formatting | bytes 2048 | tf_op jit(solution)/shard_map/reshape | solution.py:320
  2.5 61.1 %shard_map.82 = bf16[128,512]{1,0:T(8,128)(2,1)} custom-call(bf16[128,512]{1,0:T(8,128)(2,1)} %h_ref.1, bf16[1,512]{1,0:T(2,128)(2,1)} %reshape.6.pre_ref, bf16[1,512]{1,0:T(2,128)(2,1)} %reshape.7.post_ref, bf16[512,128]{1,0:T(8,128)(2,1)} %wr_ref.1, s32[8,128]{1,0:T(8,128)} %bitcast.5, bf16[128,192,512]{2,1,0:T(8,128)(2,1)} %bitcast.3, ...), custom_call_target="tpu_custom_call" | custom-call | tf_op jit(solution)/shard_map/pallas_call | solution.py:297
  63.6 1.6 %copy.10 = bf16[128,512]{1,0:T(8,128)(2,1)} copy(bf16[128,512]{1,0:T(8,128)(2,1)} %shard_map.82) | data formatting | bytes 262144

commit v2 on v1

v2 whole, which is shorter than its diff:
```python
import functools

import jax
import jax.numpy as jnp
from jax import lax
from jax.experimental import pallas as pl
from jax.experimental.pallas import tpu as pltpu
from jax.sharding import PartitionSpec as P

EPS = 1e-5
MESH = pl.DeviceIdType.MESH
BF = jnp.bfloat16
F32 = jnp.float32
EB = 8
CAP = 16
NB = 16
RING = 6
EARLY = 4
LAG_C, LAG_D = 3, 6


def remote(src, dst, send, recv, **where):
    return pltpu.make_async_remote_copy(
        src_ref=src, dst_ref=dst, send_sem=send, recv_sem=recv,
        device_id=where, device_id_type=MESH)


def kernel(model_width, h_hbm, pre_hbm, post_hbm, wr_hbm, choice_hbm, w0_ref, w1_ref, w2_ref, o_ref,
           h_ref, pre_ref, post_ref, wr_ref, choice_ref,
           ring, w2buf, oht, oh, bnorm, zsend, recv1, snd2, recv2, own2, gall, pos_ref, pt_ref,
           lbuf, lrecv1, lsnd2, lrecv2, pbuf, sq_snd, sq_recv, macc, ubuf, mrecv, mown, tq_snd, tq_recv, obuf, xbuf,
           in_sem, ring_sem, w2_sem, snd_sem, s1_r, s2_r, gy_r, gp_r, gf_r,
           l_s, l_r, sq_s, sq_r, rs_s, rs_r, tq_s, tq_r, ag_s, ag_r):
    ffn = lax.axis_index("ffn")
    emb = lax.axis_index("emb")
    core = emb % 2
    row = emb // 2
    partner = emb + 1 - 2 * core
    across = (emb + 2) % 4
    tok, width = h_ref.shape
    half = EB * CAP // 2
    quarter = half // 2

    barrier = pltpu.get_barrier_semaphore()
    for d in range(1, 4):
        pl.semaphore_signal(barrier, inc=1, device_id={"emb": (emb + d) % 4}, device_id_type=MESH)
        pl.semaphore_signal(barrier, inc=1, device_id={"ffn": (ffn + d) % 4}, device_id_type=MESH)

    loads = [pltpu.make_async_copy(a, b, in_sem.at[n]) for n, (a, b) in enumerate(
        [(h_hbm, h_ref), (choice_hbm, choice_ref), (pre_hbm, pre_ref), (wr_hbm, wr_ref), (post_hbm, post_ref)])]
    for c in loads:
        c.start()

    def ring_copies(batch):
        slot = batch % RING
        e0 = pl.ds(batch * EB, EB)
        return [
            pltpu.make_async_copy(w0_ref.at[e0, pl.ds(0, 128)], ring.at[slot, :, pl.ds(0, 128)], ring_sem.at[slot, 0]),
            pltpu.make_async_copy(w1_ref.at[e0, pl.ds(0, 128)], ring.at[slot, :, pl.ds(128, 128)], ring_sem.at[slot, 1]),
            pltpu.make_async_copy(w0_ref.at[e0, pl.ds(128, 64)], ring.at[slot, :, pl.ds(256, 64)], ring_sem.at[slot, 2]),
            pltpu.make_async_copy(w1_ref.at[e0, pl.ds(128, 64)], ring.at[slot, :, pl.ds(320, 64)], ring_sem.at[slot, 3]),
        ]

    def w2_copy(pair):
        e0 = pl.ds(pair * 2 * EB, 2 * EB)
        return pltpu.make_async_copy(w2_ref.at[e0], w2buf.at[e0], w2_sem.at[pair])

    loads[0].wait()
    for c in loads[1:]:
        c.wait()
    for b in range(RING):
        for c in ring_copies(b):
            c.start()
    for b in range(EARLY):
        w2_copy(b).start()

    hf = h_ref[...].astype(F32)
    sq = jnp.sum(hf * hf, axis=1, keepdims=True)
    sq_snd[...] = jnp.transpose(jnp.broadcast_to(sq, (tok, tok)))[0:8]

    pl.semaphore_wait(barrier, 6)

    def sq_copy(d):
        return remote(sq_snd, sq_recv.at[d - 1], sq_s.at[d - 1], sq_r.at[d - 1], emb=(emb + d) % 4)

    for d in (2, 3, 1):
        sq_copy(d).start()

    experts = lax.broadcasted_iota(jnp.int32, (tok, tok), 0)
    lanes = lax.broadcasted_iota(jnp.int32, (tok, tok), 1)
    assigned = jnp.zeros((tok, tok), F32)
    for k in range(choice_ref.shape[0]):
        assigned = assigned + (jnp.broadcast_to(choice_ref[k:k + 1, :], (tok, tok)) == experts).astype(F32)
    upper = (experts < lanes).astype(F32).astype(BF)
    before = jnp.dot(assigned.astype(BF), upper, preferred_element_type=F32)
    pos_ref[...] = jnp.where(assigned > 0.5, before, 1000.0)
    slot_no = lax.broadcasted_iota(jnp.int32, (CAP, tok), 0).astype(F32)

    def build(b, carry):
        rows = pos_ref[pl.ds(pl.multiple_of(b * 2 * EB, 2 * EB), 2 * EB), :]
        hot = jnp.concatenate(
            [(jnp.broadcast_to(rows[e:e + 1, :], (CAP, tok)) == slot_no).astype(F32) for e in range(2 * EB)], axis=0)
        oht[2 * b] = hot[0:EB * CAP].astype(BF)
        oht[2 * b + 1] = hot[EB * CAP:].astype(BF)
        oh[b] = jnp.transpose(hot).astype(BF)
        return carry

    lax.fori_loop(0, NB // 2, build, 0)
    macc[...] = jnp.zeros_like(macc)

    total = sq_snd[...]
    for d in range(1, 4):
        sq_copy(d).wait_recv()
    for d in range(1, 4):
        total = total + sq_recv[d - 1]
    inv_rows = lax.rsqrt(total / model_width + EPS)
    inv = jnp.transpose(jnp.broadcast_to(inv_rows[0:1, :], (tok, tok)))[:, 0:1]
    bnorm[...] = (h_ref[...].astype(F32) * inv * pre_ref[...].astype(F32).reshape(1, -1)).astype(BF)

    lbuf[...] = jnp.dot(bnorm[...], wr_ref[...], preferred_element_type=F32)
    htok = tok // 2
    mine = pl.ds(pl.multiple_of(core * htok, htok), htok)

    def logit_pair():
        return remote(lbuf, lrecv1, l_s.at[0], l_r.at[0], emb=partner)

    def logit_across():
        return remote(lsnd2, lrecv2, l_s.at[1], l_r.at[1], emb=across)

    def prob_pair():
        return remote(pbuf.at[mine], pbuf.at[mine], l_s.at[2], l_r.at[2], emb=partner)

    logit_pair().start()

    own_rows = pl.ds(pl.multiple_of(core * half + row * quarter, quarter), quarter)
    other_rows = pl.ds(pl.multiple_of(core * half + (1 - row) * quarter, quarter), quarter)
    pair_rows = pl.ds(pl.multiple_of((1 - core) * half, half), half)

    every = slice(None)

    def z_pair(j, r):
        return remote(zsend.at[j, pair_rows], recv1.at[j], snd_sem.at[0], r, emb=partner)

    def z_across(j, r):
        return remote(snd2.at[j], recv2.at[j], snd_sem.at[1], r, emb=across)

    def g_across(j, r):
        return remote(gall.at[j, own_rows], gall.at[j, own_rows], snd_sem.at[2], r, emb=across)

    def g_pair(j, r):
        return remote(gall.at[j, own_rows], gall.at[j, own_rows], snd_sem.at[3], r, emb=partner)

    def g_forward(j, r):
        return remote(gall.at[j, other_rows], gall.at[j, other_rows], snd_sem.at[4], r, emb=partner)

    def gather(b):
        xbuf[b % 2] = jnp.dot(oht[b], bnorm[...], preferred_element_type=F32).astype(BF)

    gather(0)

    def stage_b(j):
        z_pair(j, s1_r.at[j]).wait_recv()
        snd2[j] = (zsend[j, other_rows, :].astype(F32)
                   + recv1[j, pl.ds(pl.multiple_of((1 - row) * quarter, quarter), quarter), :].astype(F32)).astype(BF)
        z_across(j, s2_r.at[j]).start()
        own2[j] = (zsend[j, own_rows, :].astype(F32)
                   + recv1[j, pl.ds(pl.multiple_of(row * quarter, quarter), quarter), :].astype(F32))

    def stage_c(k):
        z_across(k, s2_r.at[k]).wait_recv()
        z = (own2[k] + recv2[k].astype(F32)).astype(BF).astype(F32)
        low = jax.nn.gelu(z[:, 0:128], approximate=True) * z[:, 128:256]
        mixed = z[:, 256:384]
        high = jax.nn.gelu(mixed, approximate=True) * pltpu.roll(mixed, 64, 1)
        gall[k, own_rows, 0:128] = low.astype(BF)
        gall[k, own_rows, 128:256] = high.astype(BF)
        g_across(k, gy_r.at[k]).start()
        g_pair(k, gp_r.at[k]).start()

    def stage_d(k):
        g_across(k, gy_r.at[k]).wait_recv()
        g_forward(k, gf_r.at[k]).start()

    def step(i, carry):
        slot = i % RING
        for c in ring_copies(i):
            c.wait()
        for e in range(EB):
            z = lax.dot_general(xbuf[i % 2, e * CAP:(e + 1) * CAP, :], ring[slot, e], (((1,), (1,)), ((), ())),
                                preferred_element_type=F32)
            zsend[i, e * CAP:(e + 1) * CAP, :] = z.astype(BF)
        gather(jnp.minimum(i + 1, NB - 1))
        z_pair(i, s1_r.at[i]).start()

        @pl.when(i + RING < NB)
        def _():
            for c in ring_copies(i + RING):
                c.start()

        @pl.when((i % 2 == 0) & (i // 2 + EARLY < NB // 2))
        def _():
            w2_copy(i // 2 + EARLY).start()

        @pl.when(i >= 1)
        def _():
            stage_b(i - 1)

        @pl.when(i >= LAG_C)
        def _():
            stage_c(i - LAG_C)

        @pl.when(i >= LAG_D)
        def _():
            stage_d(i - LAG_D)

        @pl.when(i == 2)
        def _():
            logit_pair().wait_recv()
            lsnd2[...] = lbuf[mine, :] + lrecv1[mine, :]
            logit_across().start()

        @pl.when(i == 5)
        def _():
            logit_across().wait_recv()
            logits = lsnd2[...] + lrecv2[...]
            pbuf[mine, :] = jax.nn.softmax(logits, axis=1)
            prob_pair().start()

        @pl.when(i == 8)
        def _():
            prob_pair().wait_recv()
            pt_ref[...] = jnp.transpose(pbuf[...])
        return carry

    lax.fori_loop(0, NB, step, 0)

    hw = width // 2
    both, first, second = slice(0, width), slice(0, hw), slice(hw, width)

    def combine(p, cols):
        macc[:, cols] += jnp.dot(oh[p], ubuf[p % 2, :, cols], preferred_element_type=F32)

    def arrived(p):
        w2_copy(p).wait()
        for b in (2 * p, 2 * p + 1):
            g_pair(b, gp_r.at[b]).wait_recv()
            g_forward(b, gf_r.at[b]).wait_recv()

    def down(p, cols):
        for e in range(2 * EB):
            b, rows = 2 * p + e // EB, slice(e % EB * CAP, (e % EB + 1) * CAP)
            probs = pt_ref[2 * p * EB + e:2 * p * EB + e + 1, :]
            gate = jnp.sum(oht[b, rows, :].astype(F32) * probs, axis=1, keepdims=True)
            y = jnp.dot(gall[b, rows, 0:192], w2buf[2 * p * EB + e, :, cols], preferred_element_type=F32)
            ubuf[p % 2, e * CAP:(e + 1) * CAP, cols] = (y.astype(BF).astype(F32) * gate).astype(BF)

    def down_both(p):
        arrived(p)
        if p:
            combine(p - 1, both)
        down(p, both)

    down_both(0)
    stage_b(NB - 1)
    stage_c(NB - 3)
    stage_d(NB - 6)
    down_both(1)
    stage_c(NB - 2)
    stage_d(NB - 5)
    down_both(2)
    stage_d(NB - 4)
    down_both(3)
    stage_c(NB - 1)
    stage_d(NB - 3)
    down_both(4)
    stage_d(NB - 2)
    down_both(5)
    stage_d(NB - 1)
    down_both(6)

    part = tok // 4

    def rs_copy(d, col):
        peer = (ffn + d) % 4
        cols = pl.ds(col * hw, hw)
        return remote(macc.at[pl.ds(pl.multiple_of(peer * part, part), part), cols], mrecv.at[d - 1, :, cols],
                      rs_s.at[d - 1, col], rs_r.at[d - 1, col], ffn=peer)

    arrived(7)
    combine(6, both)
    down(7, first)
    combine(7, first)
    for d in (2, 1, 3):
        rs_copy(d, 0).start()
    down(7, second)
    combine(7, second)
    for d in (2, 1, 3):
        rs_copy(d, 1).start()

    my_tok = pl.ds(pl.multiple_of(ffn * part, part), part)
    for c in (z_pair, z_across, g_across, g_pair, g_forward):
        c(every, s1_r.at[0]).wait_send()
    logit_pair().wait_send()
    logit_across().wait_send()
    prob_pair().wait_send()
    m = macc[my_tok, :]
    for d in range(1, 4):
        sq_copy(d).wait_send()
        rs_copy(d, 0).wait_recv()
        rs_copy(d, 1).wait_recv()
    for d in range(1, 4):
        m = m + mrecv[d - 1]
    mown[...] = m
    m2 = m * m
    tq_snd[...] = m2[:, 0:128] + m2[:, 128:256] + m2[:, 256:384] + m2[:, 384:512]

    def tq_copy(d):
        return remote(tq_snd, tq_recv.at[d - 1], tq_s.at[d - 1], tq_r.at[d - 1], emb=(emb + d) % 4)

    for d in (2, 3, 1):
        tq_copy(d).start()
    for d in range(1, 4):
        rs_copy(d, 0).wait_send()
        rs_copy(d, 1).wait_send()
        tq_copy(d).wait_recv()
    tot = tq_snd[...]
    for d in range(1, 4):
        tot = tot + tq_recv[d - 1]
    inv_post = lax.rsqrt(jnp.sum(tot, axis=1, keepdims=True) / model_width + EPS)
    res = h_ref[my_tok, :].astype(F32) + mown[...] * inv_post * post_ref[...].astype(F32).reshape(1, -1)
    obuf[...] = res.astype(BF)

    def ag_copy(d):
        return remote(obuf, o_ref.at[my_tok], ag_s.at[d - 1], ag_r.at[d - 1], ffn=(ffn + d) % 4)

    for d in (2, 1, 3):
        ag_copy(d).start()
    keep = pltpu.make_async_copy(obuf, o_ref.at[my_tok], in_sem.at[0])
    keep.start()
    for d in range(1, 4):
        tq_copy(d).wait_send()
        ag_copy(d).wait_recv()
    keep.wait()
    for d in range(1, 4):
        ag_copy(d).wait_send()


def solution(mesh):
    emb_size = mesh.shape['emb']

    def local_block(hidden, norm_pre, norm_post, w_router, w_gate, w_up, w_down, choice):
        tok, width = hidden.shape
        experts, _, fw = w_gate.shape
        dma = pltpu.SemaphoreType.DMA
        vm = pltpu.VMEM
        rows = EB * CAP
        return pl.pallas_call(
            functools.partial(kernel, width * emb_size),
            out_shape=jax.ShapeDtypeStruct((tok, width), BF),
            in_specs=[pl.BlockSpec(memory_space=pl.ANY)] * 8,
            out_specs=pl.BlockSpec(memory_space=pl.ANY),
            scratch_shapes=[
                vm((tok, width), BF), vm((width,), BF), vm((width,), BF), vm((width, experts), BF), vm((8, tok), jnp.int32),
                vm((RING, EB, 2 * fw, width), BF), vm((experts, fw, width), BF),
                vm((NB, rows, tok), BF), vm((NB // 2, tok, 2 * rows), BF), vm((tok, width), BF),
                vm((NB, rows, 2 * fw), BF), vm((NB, rows // 2, 2 * fw), BF),
                vm((NB, rows // 4, 2 * fw), BF), vm((NB, rows // 4, 2 * fw), BF), vm((NB, rows // 4, 2 * fw), F32),
                vm((NB, rows, 256), BF), vm((experts, tok), F32), vm((experts, tok), F32),
                vm((tok, experts), F32), vm((tok, experts), F32), vm((tok // 2, experts), F32),
                vm((tok // 2, experts), F32), vm((tok, experts), F32),
                vm((8, tok), F32), vm((3, 8, tok), F32),
                vm((tok, width), F32), vm((2, 2 * rows, width), BF), vm((3, tok // 4, width), F32), vm((tok // 4, width), F32),
                vm((tok // 4, 128), F32), vm((3, tok // 4, 128), F32), vm((tok // 4, width), BF), vm((2, rows, width), BF),
                dma((5,)), dma((RING, 4)), dma((NB // 2,)),
                dma((5,)), dma((NB,)), dma((NB,)), dma((NB,)), dma((NB,)), dma((NB,)),
                dma((3,)), dma((3,)), dma((3,)), dma((3,)), dma((3, 2)), dma((3, 2)), dma((3,)), dma((3,)), dma((3,)), dma((3,)),
            ],
            compiler_params=pltpu.CompilerParams(
                collective_id=0, has_side_effects=True, vmem_limit_bytes=67043328),
        )(hidden, norm_pre, norm_post, w_router, choice.T,
          jnp.swapaxes(w_gate, 1, 2), jnp.swapaxes(w_up, 1, 2), w_down)

    in_specs = (P('dp', 'emb'), P('emb'), P('emb'), P('emb', None), P(None, 'emb', 'ffn'), P(None, 'emb', 'ffn'), P(None, 'ffn', 'emb'), P('dp', None))
    return jax.shard_map(local_block, mesh=mesh, in_specs=in_specs, out_specs=P('dp', 'emb'), check_vma=False)
```

time: 65.4 us -> 55.4 us (0.85)
  Pallas kernels: 61.1 us -> 53.7 us
  local copies, waits for them, and re-layouts: 4.09 us -> 1.57 us
    pallas_call x1, Pallas kernels: 61.1 us -> 53.7 us  [local_block(): pl.pallas_call(functools.partial(kernel, width * emb_size), out_shape=jax...]
    reshape x2 -> x0, local copies, waits for them, and re-layouts: 2.53 us -> none  [the longest x1 1.27 us: local_block(): norm_post.reshape(1, width)]
where the time goes in v2:
time: 55.4 us; the launch traced here: 55.3 us
  Pallas kernels  53.7 us (97%)
  local copies, waits for them, and re-layouts  1.57 us (3%)
    pallas_call x1, Pallas kernels, local_block(): pl.pallas_call(functools.partial(kernel, width * emb_size), out_shape=jax...  53.7 us
    unnamed x1, local copies, waits for them, and re-layouts  1.57 us

profile of v2, /device:TPU:0, one launch (start us, length us, event | category | flops | bytes accessed | tf_op | source)
XLA Modules:
  0.0 55.3 jit_solution(2071103392394391947)
XLA Ops:
  0.0 53.7 %shard_map.82 = bf16[128,512]{1,0:T(8,128)(2,1)} custom-call(bf16[128,512]{1,0:T(8,128)(2,1)} %h_hbm.1, bf16[512]{0:T(512)(128)(2,1)} %pre_hbm.1, bf16[512]{0:T(512)(128)(2,1)} %post_hbm.1, bf16[512,128]{1,0:T(8,128)(2,1)} %wr_hbm.1, s32[8,128]{1,0:T(8,128)} %bitcast.5, bf16[128,192,512]{2,1,0:T(8,128)(2,1)} %bitcast.3, bf16[128,192,512]{2,1,0:T(8,128)(2,1)} %bitcast.4, ...), custom_call_target="tpu_custom_call" | custom-call | tf_op jit(solution)/shard_map/pallas_call | solution.py:357
  53.7 1.6 %copy.10 = bf16[128,512]{1,0:T(8,128)(2,1)} copy(bf16[128,512]{1,0:T(8,128)(2,1)} %shard_map.82) | data formatting | bytes 262144

commit v3 on v2

v3 whole, which is shorter than its diff:
```python
import functools

import jax
import jax.numpy as jnp
from jax import lax
from jax.experimental import pallas as pl
from jax.experimental.pallas import tpu as pltpu
from jax.sharding import PartitionSpec as P

EPS = 1e-5
MESH = pl.DeviceIdType.MESH
BF = jnp.bfloat16
F32 = jnp.float32
EB = 8
CAP = 16
NK = 8
NB = 16
QUART = 48


def remote(src, dst, send, recv, **where):
    return pltpu.make_async_remote_copy(
        src_ref=src, dst_ref=dst, send_sem=send, recv_sem=recv,
        device_id=where, device_id_type=MESH)


def kernel(model_width, h_hbm, pre_hbm, post_hbm, wr_hbm, choice_hbm, w0_ref, w1_ref, w2_ref, o_ref,
           h_ref, pre_ref, post_ref, wr_ref, choice_ref, hx_ref, cx_ref,
           w01, w2buf, oht, ohx, oh, bnorm, bother, zsend, recv1, snd2, recv2, own2, gall, gx, pos_ref, posx_ref, pt_ref,
           lbuf, lrecv1, lsnd2, lrecv2, pbuf, sq_snd, sq_recv, macc, ubuf, mrecv, mown, tq_snd, tq_recv, obuf, xbuf,
           in_sem, w01_sem, w2_sem, snd_sem, s1_r, s2_r, gy_r, gp_r, gf_r, hs_r, ha_r, f1_r, f2_r,
           l_s, l_r, x_s, x_r, sq_s, sq_r, rs_s, rs_r, tq_s, tq_r, ag_s, ag_r):
    dp = lax.axis_index("dp")
    ffn = lax.axis_index("ffn")
    emb = lax.axis_index("emb")
    xp = 1 - dp
    core = emb % 2
    row = emb // 2
    partner = emb + 1 - 2 * core
    across = (emb + 2) % 4
    tok, width = h_ref.shape
    half = EB * CAP // 2
    quarter = half // 2

    barrier = pltpu.get_barrier_semaphore()
    for d in range(1, 4):
        pl.semaphore_signal(barrier, inc=1, device_id={"ffn": (ffn + d) % 4}, device_id_type=MESH)
        pl.semaphore_signal(barrier, inc=1, device_id={"emb": (emb + d) % 4}, device_id_type=MESH)
    for d in range(4):
        pl.semaphore_signal(barrier, inc=1, device_id={"dp": xp, "emb": (emb + d) % 4}, device_id_type=MESH)

    loads = [pltpu.make_async_copy(a, b, in_sem.at[n]) for n, (a, b) in enumerate(
        [(h_hbm, h_ref), (choice_hbm, choice_ref), (pre_hbm, pre_ref), (wr_hbm, wr_ref), (post_hbm, post_ref)])]
    for c in loads:
        c.start()

    def w01_copies(k):
        e0 = pl.ds((dp * NK + k) * EB, EB)
        return [
            pltpu.make_async_copy(w0_ref.at[e0, pl.ds(0, 128)], w01.at[k, :, pl.ds(0, 128)], w01_sem.at[k, 0]),
            pltpu.make_async_copy(w1_ref.at[e0, pl.ds(0, 128)], w01.at[k, :, pl.ds(128, 128)], w01_sem.at[k, 1]),
            pltpu.make_async_copy(w0_ref.at[e0, pl.ds(128, 64)], w01.at[k, :, pl.ds(256, 64)], w01_sem.at[k, 2]),
            pltpu.make_async_copy(w1_ref.at[e0, pl.ds(128, 64)], w01.at[k, :, pl.ds(320, 64)], w01_sem.at[k, 3]),
        ]

    def pair_no(n):
        return (dp if n % 2 == 0 else xp) * (NK // 2) + n // 2

    def w2_copy(n):
        e0 = pl.ds(pair_no(n) * 2 * EB, 2 * EB)
        return pltpu.make_async_copy(w2_ref.at[e0], w2buf.at[e0], w2_sem.at[n])

    for c in loads:
        c.wait()
    for k in range(NK):
        for c in w01_copies(k):
            c.start()

    hf = h_ref[...].astype(F32)
    sq = jnp.sum(hf * hf, axis=1, keepdims=True)
    sq_snd[...] = jnp.transpose(jnp.broadcast_to(sq, (tok, tok)))[0:8]

    pl.semaphore_wait(barrier, 10)

    def sq_copy(n):
        where = dict(emb=(emb + n + 1) % 4) if n < 3 else dict(dp=xp, emb=(emb + n - 3) % 4)
        return remote(sq_snd, sq_recv.at[n], sq_s.at[n], sq_r.at[n], **where)

    def h_copy():
        return remote(h_ref, hx_ref, x_s.at[0], x_r.at[0], dp=xp)

    def c_copy():
        return remote(choice_ref, cx_ref, x_s.at[1], x_r.at[1], dp=xp)

    for n in range(7):
        sq_copy(n).start()
    c_copy().start()
    h_copy().start()

    experts = lax.broadcasted_iota(jnp.int32, (tok, tok), 0)
    lanes = lax.broadcasted_iota(jnp.int32, (tok, tok), 1)
    upper = (experts < lanes).astype(F32).astype(BF)
    slot_no = lax.broadcasted_iota(jnp.int32, (CAP, tok), 0).astype(F32)

    def slots(choices, out):
        assigned = jnp.zeros((tok, tok), F32)
        for k in range(choices.shape[0]):
            assigned = assigned + (jnp.broadcast_to(choices[k:k + 1, :], (tok, tok)) == experts).astype(F32)
        before = jnp.dot(assigned.astype(BF), upper, preferred_element_type=F32)
        out[...] = jnp.where(assigned > 0.5, before, 1000.0)

    def hot_rows(rows):
        return jnp.concatenate(
            [(jnp.broadcast_to(rows[e:e + 1, :], (CAP, tok)) == slot_no).astype(F32) for e in range(2 * EB)], axis=0)

    slots(choice_ref, pos_ref)

    def build(b, carry):
        hot = hot_rows(pos_ref[pl.ds(pl.multiple_of(b * 2 * EB, 2 * EB), 2 * EB), :])
        oht[b] = hot.astype(BF)
        oh[b] = jnp.transpose(hot).astype(BF)
        return carry

    lax.fori_loop(0, NB // 2, build, 0)
    macc[...] = jnp.zeros_like(macc)

    def normed(x, total):
        inv_rows = lax.rsqrt(total / model_width + EPS)
        inv = jnp.transpose(jnp.broadcast_to(inv_rows[0:1, :], (tok, tok)))[:, 0:1]
        return (x[...].astype(F32) * inv * pre_ref[...].astype(F32).reshape(1, -1)).astype(BF)

    for n in range(3):
        sq_copy(n).wait_recv()
    bnorm[...] = normed(h_ref, sq_snd[...] + sq_recv[0] + sq_recv[1] + sq_recv[2])

    lbuf[...] = jnp.dot(bnorm[...], wr_ref[...], preferred_element_type=F32)
    htok = tok // 2
    mine = pl.ds(pl.multiple_of(core * htok, htok), htok)

    def logit_pair():
        return remote(lbuf, lrecv1, l_s.at[0], l_r.at[0], emb=partner)

    def logit_across():
        return remote(lsnd2, lrecv2, l_s.at[1], l_r.at[1], emb=across)

    def prob_pair():
        return remote(pbuf.at[mine], pbuf.at[mine], l_s.at[2], l_r.at[2], emb=partner)

    logit_pair().start()

    own_rows = pl.ds(pl.multiple_of(core * half + row * quarter, quarter), quarter)
    other_rows = pl.ds(pl.multiple_of(core * half + (1 - row) * quarter, quarter), quarter)
    pair_rows = pl.ds(pl.multiple_of((1 - core) * half, half), half)
    own_g = pl.ds(pl.multiple_of((core * 2 + row) * QUART, 16), QUART)
    other_g = pl.ds(pl.multiple_of((core * 2 + 1 - row) * QUART, 16), QUART)

    every = slice(None)

    def z_pair(j, r):
        return remote(zsend.at[j, pair_rows], recv1.at[j], snd_sem.at[0], r, emb=partner)

    def z_across(j, r):
        return remote(snd2.at[j], recv2.at[j], snd_sem.at[1], r, emb=across)

    def at_own(k, rows):
        return gall.at[pl.ds(dp * NK, NK) if k is None else dp * NK + k, rows]

    def at_other(k, rows):
        return gall.at[pl.ds(xp * NK, NK) if k is None else xp * NK + k, rows]

    def g_across(k, r):
        return remote(at_own(k, own_g), at_own(k, own_g), snd_sem.at[2], r, emb=across)

    def g_pair(k, r):
        return remote(at_own(k, own_g), at_own(k, own_g), snd_sem.at[3], r, emb=partner)

    def g_forward(k, r):
        return remote(at_own(k, other_g), at_own(k, other_g), snd_sem.at[4], r, emb=partner)

    def x_same(k, r):
        return remote(gx if k is None else gx.at[k], at_own(k, own_g), snd_sem.at[5], r, dp=xp)

    def x_across(k, r):
        return remote(gx if k is None else gx.at[k], at_own(k, own_g), snd_sem.at[6], r, dp=xp, emb=across)

    def x_forward1(k, r):
        return remote(at_other(k, own_g), at_other(k, own_g), snd_sem.at[7], r, emb=partner)

    def x_forward2(k, r):
        return remote(at_other(k, other_g), at_other(k, other_g), snd_sem.at[8], r, emb=partner)

    rows_k = EB * CAP

    def gather_own(k):
        part_k = slice(k % 2 * rows_k, (k % 2 + 1) * rows_k)
        x = jnp.dot(oht[dp * (NK // 2) + k // 2, part_k, :], bnorm[...], preferred_element_type=F32)
        xbuf[k % 2, 0] = x.astype(BF)

    def gather_other(k):
        part_k = slice(k % 2 * rows_k, (k % 2 + 1) * rows_k)
        x = jnp.dot(ohx[k // 2, part_k, :], bother[...], preferred_element_type=F32)
        xbuf[k % 2, 1] = x.astype(BF)

    gather_own(0)

    c_copy().wait_recv()
    slots(cx_ref, posx_ref)

    def buildx(b, carry):
        at = pl.multiple_of(dp * NK * EB + b * 2 * EB, 2 * EB)
        ohx[b] = hot_rows(posx_ref[pl.ds(at, 2 * EB), :]).astype(BF)
        return carry

    lax.fori_loop(0, NK // 2, buildx, 0)
    for n in range(3, 7):
        sq_copy(n).wait_recv()
    h_copy().wait_recv()
    bother[...] = normed(hx_ref, sq_recv[3] + sq_recv[4] + sq_recv[5] + sq_recv[6])
    gather_other(0)

    def products(k):
        for c in w01_copies(k):
            c.wait()
        for e in range(EB):
            rows = slice(e * CAP, (e + 1) * CAP)
            x = jnp.concatenate([xbuf[k % 2, 0, rows, :], xbuf[k % 2, 1, rows, :]], axis=0)
            z = lax.dot_general(x, w01[k, e], (((1,), (1,)), ((), ())), preferred_element_type=F32).astype(BF)
            zsend[2 * k, rows, :] = z[0:CAP]
            zsend[2 * k + 1, rows, :] = z[CAP:]
        if k + 1 < NK:
            gather_own(k + 1)
            gather_other(k + 1)
        for j in (2 * k + 1, 2 * k):
            z_pair(j, s1_r.at[j]).start()

    def chip_sum(j):
        z_pair(j, s1_r.at[j]).wait_recv()
        snd2[j] = (zsend[j, other_rows, :].astype(F32)
                   + recv1[j, pl.ds(pl.multiple_of((1 - row) * quarter, quarter), quarter), :].astype(F32)).astype(BF)
        z_across(j, s2_r.at[j]).start()
        own2[j] = (zsend[j, own_rows, :].astype(F32)
                   + recv1[j, pl.ds(pl.multiple_of(row * quarter, quarter), quarter), :].astype(F32))

    low_lane = lax.broadcasted_iota(jnp.int32, (CAP, 128), 1) < 64

    def activation(j):
        z_across(j, s2_r.at[j]).wait_recv()
        z = (own2[j] + recv2[j].astype(F32)).astype(BF).astype(F32)
        low = (jax.nn.gelu(z[:, 0:128], approximate=True) * z[:, 128:256]).astype(BF)
        mixed = z[:, 256:384]
        high = jax.nn.gelu(mixed, approximate=True) * pltpu.roll(mixed, 64, 1)
        packed = jnp.where(low_lane, high[0:CAP], pltpu.roll(high[CAP:], 64, 1)).astype(BF)
        return jnp.concatenate([low, packed], axis=0)

    def stage_b(k):
        chip_sum(2 * k + 1)
        chip_sum(2 * k)

    def stage_c(k):
        gx[k] = activation(2 * k + 1)
        x_across(k, ha_r.at[k]).start()
        x_same(k, hs_r.at[k]).start()
        gall[dp * NK + k, own_g, :] = activation(2 * k)
        g_across(k, gy_r.at[k]).start()
        g_pair(k, gp_r.at[k]).start()

    def stage_d(k):
        g_across(k, gy_r.at[k]).wait_recv()
        g_forward(k, gf_r.at[k]).start()
        remote(gx.at[k], at_other(k, own_g), snd_sem.at[5], hs_r.at[k], dp=xp).wait_recv()
        x_forward1(k, f1_r.at[k]).start()
        remote(gx.at[k], at_other(k, other_g), snd_sem.at[6], ha_r.at[k], dp=xp, emb=across).wait_recv()
        x_forward2(k, f2_r.at[k]).start()

    hw = width // 2
    both, first, second = slice(0, width), slice(0, hw), slice(hw, width)

    def combine(n, cols):
        macc[:, cols] += jnp.dot(oh[pair_no(n)], ubuf[n % 2, :, cols], preferred_element_type=F32)

    def arrived(n):
        w2_copy(n).wait()
        for k in (n // 2 * 2, n // 2 * 2 + 1):
            if n % 2 == 0:
                g_pair(k, gp_r.at[k]).wait_recv()
                g_forward(k, gf_r.at[k]).wait_recv()
            else:
                x_forward1(k, f1_r.at[k]).wait_recv()
                x_forward2(k, f2_r.at[k]).wait_recv()

    def down(n, cols):
        p = pair_no(n)
        probs = pt_ref[pl.ds(pl.multiple_of(p * 2 * EB, 2 * EB), 2 * EB), :]
        for e in range(2 * EB):
            b, q, w = 2 * p + e // EB, e % EB // 2, e % 2
            gate = jnp.sum(oht[p, e * CAP:(e + 1) * CAP, :].astype(F32) * probs[e:e + 1, :], axis=1, keepdims=True)
            low = gall[b, q * QUART + w * CAP:q * QUART + (w + 1) * CAP, :]
            high = gall[b, q * QUART + 2 * CAP:(q + 1) * QUART, w * 64:(w + 1) * 64]
            y = jnp.dot(jnp.concatenate([low, high], axis=1), w2buf[2 * EB * p + e, :, cols], preferred_element_type=F32)
            ubuf[n % 2, e * CAP:(e + 1) * CAP, cols] = (y.astype(BF).astype(F32) * gate).astype(BF)

    def down_both(n):
        arrived(n)
        if n:
            combine(n - 1, both)
        down(n, both)

    def logits_sum():
        logit_pair().wait_recv()
        lsnd2[...] = lbuf[mine, :] + lrecv1[mine, :]
        logit_across().start()

    def probabilities():
        logit_across().wait_recv()
        logits = lsnd2[...] + lrecv2[...]
        pbuf[mine, :] = jax.nn.softmax(logits, axis=1)
        prob_pair().start()

    def gates():
        prob_pair().wait_recv()
        pt_ref[...] = jnp.transpose(pbuf[...])

    products(0)
    products(1)
    stage_b(0)
    for n in range(4):
        w2_copy(n).start()
    products(2)
    stage_b(1)
    logits_sum()
    for n in range(4, 8):
        w2_copy(n).start()
    products(3)
    stage_b(2)
    stage_c(0)
    products(4)
    stage_b(3)
    stage_c(1)
    probabilities()
    products(5)
    stage_b(4)
    stage_c(2)
    stage_d(0)
    products(6)
    stage_b(5)
    stage_c(3)
    stage_d(1)
    gates()
    products(7)
    stage_b(6)
    stage_c(4)
    stage_d(2)
    down_both(0)
    stage_b(7)
    down_both(1)
    stage_c(5)
    stage_d(3)
    down_both(2)
    stage_c(6)
    stage_d(4)
    down_both(3)
    stage_c(7)
    stage_d(5)
    down_both(4)
    stage_d(6)
    down_both(5)
    stage_d(7)
    down_both(6)

    part = tok // 4

    def rs_copy(d, col):
        peer = (ffn + d) % 4
        cols = pl.ds(col * hw, hw)
        return remote(macc.at[pl.ds(pl.multiple_of(peer * part, part), part), cols], mrecv.at[d - 1, :, cols],
                      rs_s.at[d - 1, col], rs_r.at[d - 1, col], ffn=peer)

    arrived(7)
    combine(6, both)
    down(7, first)
    combine(7, first)
    for d in (2, 1, 3):
        rs_copy(d, 0).start()
    down(7, second)
    combine(7, second)
    for d in (2, 1, 3):
        rs_copy(d, 1).start()

    my_tok = pl.ds(pl.multiple_of(ffn * part, part), part)
    for c in (z_pair, z_across):
        c(every, s1_r.at[0]).wait_send()
    for c in (g_across, g_pair, g_forward, x_same, x_across, x_forward1, x_forward2):
        c(None, gy_r.at[0]).wait_send()
    h_copy().wait_send()
    c_copy().wait_send()
    for n in range(7):
        sq_copy(n).wait_send()
    logit_pair().wait_send()
    logit_across().wait_send()
    prob_pair().wait_send()
    m = macc[my_tok, :]
    for d in range(1, 4):
        rs_copy(d, 0).wait_recv()
        rs_copy(d, 1).wait_recv()
    for d in range(1, 4):
        m = m + mrecv[d - 1]
    mown[...] = m
    m2 = m * m
    tq_snd[...] = m2[:, 0:128] + m2[:, 128:256] + m2[:, 256:384] + m2[:, 384:512]

    def tq_copy(d):
        return remote(tq_snd, tq_recv.at[d - 1], tq_s.at[d - 1], tq_r.at[d - 1], emb=(emb + d) % 4)

    for d in (2, 3, 1):
        tq_copy(d).start()
    for d in range(1, 4):
        rs_copy(d, 0).wait_send()
        rs_copy(d, 1).wait_send()
        tq_copy(d).wait_recv()
    tot = tq_snd[...]
    for d in range(1, 4):
        tot = tot + tq_recv[d - 1]
    inv_post = lax.rsqrt(jnp.sum(tot, axis=1, keepdims=True) / model_width + EPS)
    res = h_ref[my_tok, :].astype(F32) + mown[...] * inv_post * post_ref[...].astype(F32).reshape(1, -1)
    obuf[...] = res.astype(BF)

    def ag_copy(d):
        return remote(obuf, o_ref.at[my_tok], ag_s.at[d - 1], ag_r.at[d - 1], ffn=(ffn + d) % 4)

    for d in (2, 1, 3):
        ag_copy(d).start()
    keep = pltpu.make_async_copy(obuf, o_ref.at[my_tok], in_sem.at[0])
    keep.start()
    for d in range(1, 4):
        tq_copy(d).wait_send()
        ag_copy(d).wait_recv()
    keep.wait()
    for d in range(1, 4):
        ag_copy(d).wait_send()


def solution(mesh):
    emb_size = mesh.shape['emb']

    def local_block(hidden, norm_pre, norm_post, w_router, w_gate, w_up, w_down, choice):
        tok, width = hidden.shape
        experts, _, fw = w_gate.shape
        dma = pltpu.SemaphoreType.DMA
        vm = pltpu.VMEM
        rows = EB * CAP
        return pl.pallas_call(
            functools.partial(kernel, width * emb_size),
            out_shape=jax.ShapeDtypeStruct((tok, width), BF),
            in_specs=[pl.BlockSpec(memory_space=pl.ANY)] * 8,
            out_specs=pl.BlockSpec(memory_space=pl.ANY),
            scratch_shapes=[
                vm((tok, width), BF), vm((width,), BF), vm((width,), BF), vm((width, experts), BF), vm((8, tok), jnp.int32),
                vm((tok, width), BF), vm((8, tok), jnp.int32),
                vm((NK, EB, 2 * fw, width), BF), vm((experts, fw, width), BF),
                vm((NB // 2, 2 * rows, tok), BF), vm((NK // 2, 2 * rows, tok), BF), vm((NB // 2, tok, 2 * rows), BF),
                vm((tok, width), BF), vm((tok, width), BF),
                vm((NB, rows, 2 * fw), BF), vm((NB, rows // 2, 2 * fw), BF),
                vm((NB, rows // 4, 2 * fw), BF), vm((NB, rows // 4, 2 * fw), BF), vm((NB, rows // 4, 2 * fw), F32),
                vm((NB, 4 * QUART, 128), BF), vm((NK, QUART, 128), BF),
                vm((experts, tok), F32), vm((experts, tok), F32), vm((experts, tok), F32),
                vm((tok, experts), F32), vm((tok, experts), F32), vm((tok // 2, experts), F32),
                vm((tok // 2, experts), F32), vm((tok, experts), F32),
                vm((8, tok), F32), vm((7, 8, tok), F32),
                vm((tok, width), F32), vm((2, 2 * rows, width), BF), vm((3, tok // 4, width), F32), vm((tok // 4, width), F32),
                vm((tok // 4, 128), F32), vm((3, tok // 4, 128), F32), vm((tok // 4, width), BF), vm((2, 2, rows, width), BF),
                dma((5,)), dma((NK, 4)), dma((NB // 2,)),
                dma((9,)), dma((NB,)), dma((NB,)), dma((NK,)), dma((NK,)), dma((NK,)), dma((NK,)), dma((NK,)), dma((NK,)), dma((NK,)),
                dma((3,)), dma((3,)), dma((2,)), dma((2,)), dma((7,)), dma((7,)),
                dma((3, 2)), dma((3, 2)), dma((3,)), dma((3,)), dma((3,)), dma((3,)),
            ],
            compiler_params=pltpu.CompilerParams(
                collective_id=0, has_side_effects=True, vmem_limit_bytes=67043328),
        )(hidden, norm_pre, norm_post, w_router, choice.T,
          jnp.swapaxes(w_gate, 1, 2), jnp.swapaxes(w_up, 1, 2), w_down)

    in_specs = (P('dp', 'emb'), P('emb'), P('emb'), P('emb', None), P(None, 'emb', 'ffn'), P(None, 'emb', 'ffn'), P(None, 'ffn', 'emb'), P('dp', None))
    return jax.shard_map(local_block, mesh=mesh, in_specs=in_specs, out_specs=P('dp', 'emb'), check_vma=False)
```

time: 55.4 us -> 51.9 us (0.937)
  Pallas kernels: 53.7 us -> 50.2 us
    pallas_call x1, Pallas kernels: 53.7 us -> 50.2 us  [local_block(): pl.pallas_call(functools.partial(kernel, width * emb_size), out_shape=jax...]
where the time goes in v3:
time: 51.9 us; the launch traced here: 51.8 us
  Pallas kernels  50.2 us (97%)
  local copies, waits for them, and re-layouts  1.57 us (3%)
    pallas_call x1, Pallas kernels, local_block(): pl.pallas_call(functools.partial(kernel, width * emb_size), out_shape=jax...  50.2 us
    unnamed x1, local copies, waits for them, and re-layouts  1.57 us

profile of v3, /device:TPU:0, one launch (start us, length us, event | category | flops | bytes accessed | tf_op | source)
XLA Modules:
  0.0 51.8 jit_solution(5738979914601252979)
XLA Ops:
  0.0 50.2 %shard_map.82 = bf16[128,512]{1,0:T(8,128)(2,1)} custom-call(bf16[128,512]{1,0:T(8,128)(2,1)} %h_hbm.1, bf16[512]{0:T(512)(128)(2,1)} %pre_hbm.1, bf16[512]{0:T(512)(128)(2,1)} %post_hbm.1, bf16[512,128]{1,0:T(8,128)(2,1)} %wr_hbm.1, s32[8,128]{1,0:T(8,128)} %bitcast.5, bf16[128,192,512]{2,1,0:T(8,128)(2,1)} %bitcast.3, bf16[128,192,512]{2,1,0:T(8,128)(2,1)} %bitcast.4, ...), custom_call_target="tpu_custom_call" | custom-call | tf_op jit(solution)/shard_map/pallas_call | solution.py:451
  50.2 1.6 %copy.10 = bf16[128,512]{1,0:T(8,128)(2,1)} copy(bf16[128,512]{1,0:T(8,128)(2,1)} %shard_map.82) | data formatting | bytes 262144

commit v4 on v3

--- a/solution.py
+++ b/solution.py
@@ -15,6 +15,7 @@
 CAP = 16
 NK = 8
 NB = 16
+DIRECT = 7
 QUART = 48
 
 
@@ -28,7 +29,7 @@
            h_ref, pre_ref, post_ref, wr_ref, choice_ref, hx_ref, cx_ref,
            w01, w2buf, oht, ohx, oh, bnorm, bother, zsend, recv1, snd2, recv2, own2, gall, gx, pos_ref, posx_ref, pt_ref,
            lbuf, lrecv1, lsnd2, lrecv2, pbuf, sq_snd, sq_recv, macc, ubuf, mrecv, mown, tq_snd, tq_recv, obuf, xbuf,
-           in_sem, w01_sem, w2_sem, snd_sem, s1_r, s2_r, gy_r, gp_r, gf_r, hs_r, ha_r, f1_r, f2_r,
+           in_sem, w_sem, snd_sem, s1_r, s2_r, gy_r, hs_r, ha_r, ga_r,
            l_s, l_r, x_s, x_r, sq_s, sq_r, rs_s, rs_r, tq_s, tq_r, ag_s, ag_r):
     dp = lax.axis_index("dp")
     ffn = lax.axis_index("ffn")
@@ -54,28 +55,25 @@
     for c in loads:
         c.start()
 
-    def w01_copies(k):
+    def w01_start(k):
         e0 = pl.ds((dp * NK + k) * EB, EB)
-        return [
-            pltpu.make_async_copy(w0_ref.at[e0, pl.ds(0, 128)], w01.at[k, :, pl.ds(0, 128)], w01_sem.at[k, 0]),
-            pltpu.make_async_copy(w1_ref.at[e0, pl.ds(0, 128)], w01.at[k, :, pl.ds(128, 128)], w01_sem.at[k, 1]),
-            pltpu.make_async_copy(w0_ref.at[e0, pl.ds(128, 64)], w01.at[k, :, pl.ds(256, 64)], w01_sem.at[k, 2]),
-            pltpu.make_async_copy(w1_ref.at[e0, pl.ds(128, 64)], w01.at[k, :, pl.ds(320, 64)], w01_sem.at[k, 3]),
-        ]
+        pltpu.make_async_copy(w0_ref.at[e0, pl.ds(0, 128)], w01.at[k, :, pl.ds(0, 128)], w_sem.at[k]).start()
+        pltpu.make_async_copy(w1_ref.at[e0, pl.ds(0, 128)], w01.at[k, :, pl.ds(128, 128)], w_sem.at[k]).start()
+        pltpu.make_async_copy(w0_ref.at[e0, pl.ds(128, 64)], w01.at[k, :, pl.ds(256, 64)], w_sem.at[k]).start()
+        pltpu.make_async_copy(w1_ref.at[e0, pl.ds(128, 64)], w01.at[k, :, pl.ds(320, 64)], w_sem.at[k]).start()
+
+    def w01_wait(k):
+        pltpu.make_async_copy(w01.at[k], w01.at[k], w_sem.at[k]).wait()
 
     def pair_no(n):
         return (dp if n % 2 == 0 else xp) * (NK // 2) + n // 2
 
     def w2_copy(n):
         e0 = pl.ds(pair_no(n) * 2 * EB, 2 * EB)
-        return pltpu.make_async_copy(w2_ref.at[e0], w2buf.at[e0], w2_sem.at[n])
+        return pltpu.make_async_copy(w2_ref.at[e0], w2buf.at[e0], w_sem.at[n])
 
     for c in loads:
         c.wait()
-    for k in range(NK):
-        for c in w01_copies(k):
-            c.start()
-
     hf = h_ref[...].astype(F32)
     sq = jnp.sum(hf * hf, axis=1, keepdims=True)
     sq_snd[...] = jnp.transpose(jnp.broadcast_to(sq, (tok, tok)))[0:8]
@@ -84,7 +82,7 @@
 
     def sq_copy(n):
         where = dict(emb=(emb + n + 1) % 4) if n < 3 else dict(dp=xp, emb=(emb + n - 3) % 4)
-        return remote(sq_snd, sq_recv.at[n], sq_s.at[n], sq_r.at[n], **where)
+        return remote(sq_snd, sq_recv.at[n], sq_s.at[0], sq_r.at[0 if n < 3 else 1], **where)
 
     def h_copy():
         return remote(h_ref, hx_ref, x_s.at[0], x_r.at[0], dp=xp)
@@ -96,6 +94,8 @@
         sq_copy(n).start()
     c_copy().start()
     h_copy().start()
+    for k in range(NK):
+        w01_start(k)
 
     experts = lax.broadcasted_iota(jnp.int32, (tok, tok), 0)
     lanes = lax.broadcasted_iota(jnp.int32, (tok, tok), 1)
@@ -129,8 +129,7 @@
         inv = jnp.transpose(jnp.broadcast_to(inv_rows[0:1, :], (tok, tok)))[:, 0:1]
         return (x[...].astype(F32) * inv * pre_ref[...].astype(F32).reshape(1, -1)).astype(BF)
 
-    for n in range(3):
-        sq_copy(n).wait_recv()
+    remote(sq_snd, sq_recv.at[pl.ds(0, 3)], sq_s.at[0], sq_r.at[0], emb=across).wait_recv()
     bnorm[...] = normed(h_ref, sq_snd[...] + sq_recv[0] + sq_recv[1] + sq_recv[2])
 
     lbuf[...] = jnp.dot(bnorm[...], wr_ref[...], preferred_element_type=F32)
@@ -156,38 +155,23 @@
 
     every = slice(None)
 
-    def z_pair(j, r):
-        return remote(zsend.at[j, pair_rows], recv1.at[j], snd_sem.at[0], r, emb=partner)
-
-    def z_across(j, r):
-        return remote(snd2.at[j], recv2.at[j], snd_sem.at[1], r, emb=across)
-
-    def at_own(k, rows):
-        return gall.at[pl.ds(dp * NK, NK) if k is None else dp * NK + k, rows]
-
-    def at_other(k, rows):
-        return gall.at[pl.ds(xp * NK, NK) if k is None else xp * NK + k, rows]
-
-    def g_across(k, r):
-        return remote(at_own(k, own_g), at_own(k, own_g), snd_sem.at[2], r, emb=across)
-
-    def g_pair(k, r):
-        return remote(at_own(k, own_g), at_own(k, own_g), snd_sem.at[3], r, emb=partner)
-
-    def g_forward(k, r):
-        return remote(at_own(k, other_g), at_own(k, other_g), snd_sem.at[4], r, emb=partner)
-
-    def x_same(k, r):
-        return remote(gx if k is None else gx.at[k], at_own(k, own_g), snd_sem.at[5], r, dp=xp)
-
-    def x_across(k, r):
-        return remote(gx if k is None else gx.at[k], at_own(k, own_g), snd_sem.at[6], r, dp=xp, emb=across)
-
-    def x_forward1(k, r):
-        return remote(at_other(k, own_g), at_other(k, own_g), snd_sem.at[7], r, emb=partner)
-
-    def x_forward2(k, r):
-        return remote(at_other(k, other_g), at_other(k, other_g), snd_sem.at[8], r, emb=partner)
+    def z_pair(k, r):
+        return remote(zsend.at[k, :, pair_rows], recv1.at[k], snd_sem.at[0], r, emb=partner)
+
+    def z_across(k, r):
+        return remote(snd2.at[k], recv2.at[k], snd_sem.at[1], r, emb=across)
+
+    def g_at(x, k, rows, count=None):
+        return gall.at[x * NK + k if count is None else pl.ds(x * NK + k, count), rows]
+
+    def g_copy(sem, r, x, rows, k, count=None, **where):
+        return remote(g_at(x, k, rows, count), g_at(x, k, rows, count), snd_sem.at[sem], r, **where)
+
+    def x_copy(sem, r, k, count=None, **where):
+        return remote(gx.at[k if count is None else pl.ds(k, count)], g_at(dp, k, own_g, count), snd_sem.at[sem], r, dp=xp, **where)
+
+    theirs = pl.ds(pl.multiple_of((1 - core) * 2 * QUART, 16), 2 * QUART)
+    corner = 3 - emb
 
     rows_k = EB * CAP
 
@@ -212,65 +196,72 @@
         return carry
 
     lax.fori_loop(0, NK // 2, buildx, 0)
-    for n in range(3, 7):
-        sq_copy(n).wait_recv()
+    remote(sq_snd, sq_recv.at[pl.ds(3, 4)], sq_s.at[0], sq_r.at[1], dp=xp).wait_recv()
     h_copy().wait_recv()
     bother[...] = normed(hx_ref, sq_recv[3] + sq_recv[4] + sq_recv[5] + sq_recv[6])
     gather_other(0)
 
     def products(k):
-        for c in w01_copies(k):
-            c.wait()
+        w01_wait(k)
         for e in range(EB):
             rows = slice(e * CAP, (e + 1) * CAP)
             x = jnp.concatenate([xbuf[k % 2, 0, rows, :], xbuf[k % 2, 1, rows, :]], axis=0)
             z = lax.dot_general(x, w01[k, e], (((1,), (1,)), ((), ())), preferred_element_type=F32).astype(BF)
-            zsend[2 * k, rows, :] = z[0:CAP]
-            zsend[2 * k + 1, rows, :] = z[CAP:]
+            zsend[k, 0, rows, :] = z[0:CAP]
+            zsend[k, 1, rows, :] = z[CAP:]
         if k + 1 < NK:
             gather_own(k + 1)
             gather_other(k + 1)
-        for j in (2 * k + 1, 2 * k):
-            z_pair(j, s1_r.at[j]).start()
-
-    def chip_sum(j):
-        z_pair(j, s1_r.at[j]).wait_recv()
-        snd2[j] = (zsend[j, other_rows, :].astype(F32)
-                   + recv1[j, pl.ds(pl.multiple_of((1 - row) * quarter, quarter), quarter), :].astype(F32)).astype(BF)
-        z_across(j, s2_r.at[j]).start()
-        own2[j] = (zsend[j, own_rows, :].astype(F32)
-                   + recv1[j, pl.ds(pl.multiple_of(row * quarter, quarter), quarter), :].astype(F32))
+        z_pair(k, s1_r.at[k]).start()
+        w2_copy(k).start()
+
+    def stage_b(k):
+        z_pair(k, s1_r.at[k]).wait_recv()
+        near = pl.ds(pl.multiple_of(row * quarter, quarter), quarter)
+        far = pl.ds(pl.multiple_of((1 - row) * quarter, quarter), quarter)
+        snd2[k] = (zsend[k, :, other_rows, :].astype(F32) + recv1[k, :, far, :].astype(F32)).astype(BF)
+        z_across(k, s2_r.at[k]).start()
+        own2[k] = zsend[k, :, own_rows, :].astype(F32) + recv1[k, :, near, :].astype(F32)
 
     low_lane = lax.broadcasted_iota(jnp.int32, (CAP, 128), 1) < 64
 
-    def activation(j):
-        z_across(j, s2_r.at[j]).wait_recv()
-        z = (own2[j] + recv2[j].astype(F32)).astype(BF).astype(F32)
+    def activation(k, g):
+        z = (own2[k, g] + recv2[k, g].astype(F32)).astype(BF).astype(F32)
         low = (jax.nn.gelu(z[:, 0:128], approximate=True) * z[:, 128:256]).astype(BF)
         mixed = z[:, 256:384]
         high = jax.nn.gelu(mixed, approximate=True) * pltpu.roll(mixed, 64, 1)
         packed = jnp.where(low_lane, high[0:CAP], pltpu.roll(high[CAP:], 64, 1)).astype(BF)
         return jnp.concatenate([low, packed], axis=0)
 
-    def stage_b(k):
-        chip_sum(2 * k + 1)
-        chip_sum(2 * k)
-
     def stage_c(k):
-        gx[k] = activation(2 * k + 1)
-        x_across(k, ha_r.at[k]).start()
-        x_same(k, hs_r.at[k]).start()
-        gall[dp * NK + k, own_g, :] = activation(2 * k)
-        g_across(k, gy_r.at[k]).start()
-        g_pair(k, gp_r.at[k]).start()
+        n = k // 2 * 2
+        z_across(k, s2_r.at[k]).wait_recv()
+        gx[k] = activation(k, 1)
+        x_copy(6, ha_r.at[k], k, emb=across).start()
+        x_copy(5, hs_r.at[k], k).start()
+        if k >= DIRECT:
+            x_copy(9, ga_r.at[n + 1], k, emb=corner).start()
+            x_copy(10, ga_r.at[n + 1], k, emb=partner).start()
+        gall[dp * NK + k, own_g, :] = activation(k, 0)
+        g_copy(2, gy_r.at[k], dp, own_g, k, emb=across).start()
+        g_copy(3, ga_r.at[n], dp, own_g, k, emb=partner).start()
+        if k >= DIRECT:
+            g_copy(11, ga_r.at[n], dp, own_g, k, emb=corner).start()
+
+    def from_across(k):
+        return g_copy(2, gy_r.at[k], dp, other_g, k, emb=across)
+
+    def from_x(k, rows, r):
+        return g_copy(5, r, xp, rows, k, dp=xp)
 
     def stage_d(k):
-        g_across(k, gy_r.at[k]).wait_recv()
-        g_forward(k, gf_r.at[k]).start()
-        remote(gx.at[k], at_other(k, own_g), snd_sem.at[5], hs_r.at[k], dp=xp).wait_recv()
-        x_forward1(k, f1_r.at[k]).start()
-        remote(gx.at[k], at_other(k, other_g), snd_sem.at[6], ha_r.at[k], dp=xp, emb=across).wait_recv()
-        x_forward2(k, f2_r.at[k]).start()
+        n = k // 2 * 2
+        from_across(k).wait_recv()
+        g_copy(4, ga_r.at[n], dp, other_g, k, emb=partner).start()
+        from_x(k, own_g, hs_r.at[k]).wait_recv()
+        g_copy(7, ga_r.at[n + 1], xp, own_g, k, emb=partner).start()
+        from_x(k, other_g, ha_r.at[k]).wait_recv()
+        g_copy(8, ga_r.at[n + 1], xp, other_g, k, emb=partner).start()
 
     hw = width // 2
     both, first, second = slice(0, width), slice(0, hw), slice(hw, width)
@@ -281,12 +272,12 @@
     def arrived(n):
         w2_copy(n).wait()
         for k in (n // 2 * 2, n // 2 * 2 + 1):
-            if n % 2 == 0:
-                g_pair(k, gp_r.at[k]).wait_recv()
-                g_forward(k, gf_r.at[k]).wait_recv()
-            else:
-                x_forward1(k, f1_r.at[k]).wait_recv()
-                x_forward2(k, f2_r.at[k]).wait_recv()
+            if k >= DIRECT and n % 2 == 0:
+                from_across(k).wait_recv()
+            if k >= DIRECT and n % 2 == 1:
+                from_x(k, own_g, hs_r.at[k]).wait_recv()
+                from_x(k, other_g, ha_r.at[k]).wait_recv()
+        g_copy(3, ga_r.at[n], dp if n % 2 == 0 else xp, theirs, n // 2 * 2, 2, emb=partner).wait_recv()
 
     def down(n, cols):
         p = pair_no(n)
@@ -323,13 +314,9 @@
     products(0)
     products(1)
     stage_b(0)
-    for n in range(4):
-        w2_copy(n).start()
     products(2)
     stage_b(1)
     logits_sum()
-    for n in range(4, 8):
-        w2_copy(n).start()
     products(3)
     stage_b(2)
     stage_c(0)
@@ -352,19 +339,18 @@
     stage_d(2)
     down_both(0)
     stage_b(7)
-    down_both(1)
     stage_c(5)
     stage_d(3)
+    down_both(1)
+    stage_d(4)
+    stage_c(6)
     down_both(2)
-    stage_c(6)
-    stage_d(4)
-    down_both(3)
     stage_c(7)
     stage_d(5)
+    down_both(3)
     down_both(4)
     stage_d(6)
     down_both(5)
-    stage_d(7)
     down_both(6)
 
     part = tok // 4
@@ -373,7 +359,7 @@
         peer = (ffn + d) % 4
         cols = pl.ds(col * hw, hw)
         return remote(macc.at[pl.ds(pl.multiple_of(peer * part, part), part), cols], mrecv.at[d - 1, :, cols],
-                      rs_s.at[d - 1, col], rs_r.at[d - 1, col], ffn=peer)
+                      rs_s.at[0], rs_r.at[col], ffn=peer)
 
     arrived(7)
     combine(6, both)
@@ -389,19 +375,21 @@
     my_tok = pl.ds(pl.multiple_of(ffn * part, part), part)
     for c in (z_pair, z_across):
         c(every, s1_r.at[0]).wait_send()
-    for c in (g_across, g_pair, g_forward, x_same, x_across, x_forward1, x_forward2):
-        c(None, gy_r.at[0]).wait_send()
+    for sem, x, rows, k, count in ((2, dp, own_g, 0, NK), (3, dp, own_g, 0, NK), (4, dp, other_g, 0, DIRECT),
+                                   (7, xp, own_g, 0, DIRECT), (8, xp, other_g, 0, DIRECT), (11, dp, own_g, DIRECT, NK - DIRECT)):
+        g_copy(sem, gy_r.at[0], x, rows, k, count, emb=partner).wait_send()
+    for sem, k, count in ((5, 0, NK), (6, 0, NK), (9, DIRECT, NK - DIRECT), (10, DIRECT, NK - DIRECT)):
+        x_copy(sem, gy_r.at[0], k, count).wait_send()
     h_copy().wait_send()
     c_copy().wait_send()
-    for n in range(7):
-        sq_copy(n).wait_send()
+    remote(sq_recv, sq_recv, sq_s.at[0], sq_r.at[0], dp=xp).wait_send()
     logit_pair().wait_send()
     logit_across().wait_send()
     prob_pair().wait_send()
     m = macc[my_tok, :]
-    for d in range(1, 4):
-        rs_copy(d, 0).wait_recv()
-        rs_copy(d, 1).wait_recv()
+    for col in range(2):
+        all_in = mrecv.at[:, :, pl.ds(col * hw, hw)]
+        remote(all_in, all_in, rs_s.at[0], rs_r.at[col], ffn=(ffn + 1) % 4).wait_recv()
     for d in range(1, 4):
         m = m + mrecv[d - 1]
     mown[...] = m
@@ -409,14 +397,12 @@
     tq_snd[...] = m2[:, 0:128] + m2[:, 128:256] + m2[:, 256:384] + m2[:, 384:512]
 
     def tq_copy(d):
-        return remote(tq_snd, tq_recv.at[d - 1], tq_s.at[d - 1], tq_r.at[d - 1], emb=(emb + d) % 4)
+        return remote(tq_snd, tq_recv.at[d - 1], tq_s.at[0], tq_r.at[0], emb=(emb + d) % 4)
 
     for d in (2, 3, 1):
         tq_copy(d).start()
-    for d in range(1, 4):
-        rs_copy(d, 0).wait_send()
-        rs_copy(d, 1).wait_send()
-        tq_copy(d).wait_recv()
+    remote(mrecv, mrecv, rs_s.at[0], rs_r.at[0], ffn=(ffn + 1) % 4).wait_send()
+    remote(tq_recv, tq_recv, tq_s.at[0], tq_r.at[0], emb=partner).wait()
     tot = tq_snd[...]
     for d in range(1, 4):
         tot = tot + tq_recv[d - 1]
@@ -425,18 +411,15 @@
     obuf[...] = res.astype(BF)
 
     def ag_copy(d):
-        return remote(obuf, o_ref.at[my_tok], ag_s.at[d - 1], ag_r.at[d - 1], ffn=(ffn + d) % 4)
+        return remote(obuf, o_ref.at[my_tok], ag_s.at[0], ag_r.at[0], ffn=(ffn + d) % 4)
 
     for d in (2, 1, 3):
         ag_copy(d).start()
     keep = pltpu.make_async_copy(obuf, o_ref.at[my_tok], in_sem.at[0])
     keep.start()
-    for d in range(1, 4):
-        tq_copy(d).wait_send()
-        ag_copy(d).wait_recv()
+    others = o_ref.at[pl.ds(0, 3 * part)]
     keep.wait()
-    for d in range(1, 4):
-        ag_copy(d).wait_send()
+    remote(others, others, ag_s.at[0], ag_r.at[0], ffn=(ffn + 1) % 4).wait()
 
 
 def solution(mesh):
@@ -459,8 +442,8 @@
                 vm((NK, EB, 2 * fw, width), BF), vm((experts, fw, width), BF),
                 vm((NB // 2, 2 * rows, tok), BF), vm((NK // 2, 2 * rows, tok), BF), vm((NB // 2, tok, 2 * rows), BF),
                 vm((tok, width), BF), vm((tok, width), BF),
-                vm((NB, rows, 2 * fw), BF), vm((NB, rows // 2, 2 * fw), BF),
-                vm((NB, rows // 4, 2 * fw), BF), vm((NB, rows // 4, 2 * fw), BF), vm((NB, rows // 4, 2 * fw), F32),
+                vm((NK, 2, rows, 2 * fw), BF), vm((NK, 2, rows // 2, 2 * fw), BF),
+                vm((NK, 2, rows // 4, 2 * fw), BF), vm((NK, 2, rows // 4, 2 * fw), BF), vm((NK, 2, rows // 4, 2 * fw), F32),
                 vm((NB, 4 * QUART, 128), BF), vm((NK, QUART, 128), BF),
                 vm((experts, tok), F32), vm((experts, tok), F32), vm((experts, tok), F32),
                 vm((tok, experts), F32), vm((tok, experts), F32), vm((tok // 2, experts), F32),
@@ -468,10 +451,9 @@
                 vm((8, tok), F32), vm((7, 8, tok), F32),
                 vm((tok, width), F32), vm((2, 2 * rows, width), BF), vm((3, tok // 4, width), F32), vm((tok // 4, width), F32),
                 vm((tok // 4, 128), F32), vm((3, tok // 4, 128), F32), vm((tok // 4, width), BF), vm((2, 2, rows, width), BF),
-                dma((5,)), dma((NK, 4)), dma((NB // 2,)),
-                dma((9,)), dma((NB,)), dma((NB,)), dma((NK,)), dma((NK,)), dma((NK,)), dma((NK,)), dma((NK,)), dma((NK,)), dma((NK,)),
-                dma((3,)), dma((3,)), dma((2,)), dma((2,)), dma((7,)), dma((7,)),
-                dma((3, 2)), dma((3, 2)), dma((3,)), dma((3,)), dma((3,)), dma((3,)),
+                dma((5,)), dma((NK,)), dma((12,)), dma((NK,)), dma((NK,)), dma((NK,)), dma((NK,)), dma((NK,)), dma((NK,)),
+                dma((3,)), dma((3,)), dma((2,)), dma((2,)), dma((1,)), dma((2,)),
+                dma((1,)), dma((2,)), dma((1,)), dma((1,)), dma((1,)), dma((1,)),
             ],
             compiler_params=pltpu.CompilerParams(
                 collective_id=0, has_side_effects=True, vmem_limit_bytes=67043328),

time: 51.9 us -> 50 us (0.963)
  Pallas kernels: 50.2 us -> 48.3 us
    pallas_call x1, Pallas kernels: 50.2 us -> 48.3 us  [local_block(): pl.pallas_call(functools.partial(kernel, width * emb_size), out_shape=jax...]
where the time goes in v4:
time: 50 us; the launch traced here: 49.9 us
  Pallas kernels  48.3 us (97%)
  local copies, waits for them, and re-layouts  1.57 us (3%)
    pallas_call x1, Pallas kernels, local_block(): pl.pallas_call(functools.partial(kernel, width * emb_size), out_shape=jax...  48.3 us
    unnamed x1, local copies, waits for them, and re-layouts  1.57 us

profile of v4, /device:TPU:0, one launch (start us, length us, event | category | flops | bytes accessed | tf_op | source)
XLA Modules:
  0.0 49.9 jit_solution(12959793166066847517)
XLA Ops:
  0.0 48.3 %shard_map.82 = bf16[128,512]{1,0:T(8,128)(2,1)} custom-call(bf16[128,512]{1,0:T(8,128)(2,1)} %h_hbm.1, bf16[512]{0:T(512)(128)(2,1)} %pre_hbm.1, bf16[512]{0:T(512)(128)(2,1)} %post_hbm.1, bf16[512,128]{1,0:T(8,128)(2,1)} %wr_hbm.1, s32[8,128]{1,0:T(8,128)} %bitcast.5, bf16[128,192,512]{2,1,0:T(8,128)(2,1)} %bitcast.3, bf16[128,192,512]{2,1,0:T(8,128)(2,1)} %bitcast.4, ...), custom_call_target="tpu_custom_call" | custom-call | tf_op jit(solution)/shard_map/pallas_call | solution.py:434
  48.3 1.6 %copy.10 = bf16[128,512]{1,0:T(8,128)(2,1)} copy(bf16[128,512]{1,0:T(8,128)(2,1)} %shard_map.82) | data formatting | bytes 262144

commit v5 on v4

--- a/solution.py
+++ b/solution.py
@@ -11,6 +11,7 @@
 MESH = pl.DeviceIdType.MESH
 BF = jnp.bfloat16
 F32 = jnp.float32
+LANES = 128
 EB = 8
 CAP = 16
 NK = 8
@@ -74,26 +75,26 @@
 
     for c in loads:
         c.wait()
+    pl.semaphore_wait(barrier, 10)
+
+    def sq_copy(n):
+        where = dict(emb=(emb + n + 1) % 4) if n < 3 else dict(dp=xp, emb=(emb + n - 3) % 4)
+        return remote(sq_snd, sq_recv.at[n], sq_s, sq_r.at[0 if n < 3 else 1], **where)
+
+    def h_copy():
+        return remote(h_ref, hx_ref, x_s.at[0], x_r.at[0], dp=xp)
+
+    def c_copy():
+        return remote(choice_ref, cx_ref, x_s.at[1], x_r.at[1], dp=xp)
+
+    c_copy().start()
+    h_copy().start()
+
     hf = h_ref[...].astype(F32)
     sq = jnp.sum(hf * hf, axis=1, keepdims=True)
     sq_snd[...] = jnp.transpose(jnp.broadcast_to(sq, (tok, tok)))[0:8]
-
-    pl.semaphore_wait(barrier, 10)
-
-    def sq_copy(n):
-        where = dict(emb=(emb + n + 1) % 4) if n < 3 else dict(dp=xp, emb=(emb + n - 3) % 4)
-        return remote(sq_snd, sq_recv.at[n], sq_s.at[0], sq_r.at[0 if n < 3 else 1], **where)
-
-    def h_copy():
-        return remote(h_ref, hx_ref, x_s.at[0], x_r.at[0], dp=xp)
-
-    def c_copy():
-        return remote(choice_ref, cx_ref, x_s.at[1], x_r.at[1], dp=xp)
-
     for n in range(7):
         sq_copy(n).start()
-    c_copy().start()
-    h_copy().start()
     for k in range(NK):
         w01_start(k)
 
@@ -129,8 +130,8 @@
         inv = jnp.transpose(jnp.broadcast_to(inv_rows[0:1, :], (tok, tok)))[:, 0:1]
         return (x[...].astype(F32) * inv * pre_ref[...].astype(F32).reshape(1, -1)).astype(BF)
 
-    remote(sq_snd, sq_recv.at[pl.ds(0, 3)], sq_s.at[0], sq_r.at[0], emb=across).wait_recv()
-    bnorm[...] = normed(h_ref, sq_snd[...] + sq_recv[0] + sq_recv[1] + sq_recv[2])
+    remote(sq_snd, sq_recv.at[pl.ds(0, 3)], sq_s, sq_r.at[0], emb=across).wait_recv()
+    bnorm[...] = normed(h_ref, functools.reduce(lax.add, [sq_recv[n] for n in range(3)], sq_snd[...]))
 
     lbuf[...] = jnp.dot(bnorm[...], wr_ref[...], preferred_element_type=F32)
     htok = tok // 2
@@ -155,11 +156,11 @@
 
     every = slice(None)
 
-    def z_pair(k, r):
-        return remote(zsend.at[k, :, pair_rows], recv1.at[k], snd_sem.at[0], r, emb=partner)
-
-    def z_across(k, r):
-        return remote(snd2.at[k], recv2.at[k], snd_sem.at[1], r, emb=across)
+    def z_pair(k, r, g=every):
+        return remote(zsend.at[k, g, pair_rows], recv1.at[k, g], snd_sem.at[0], r, emb=partner)
+
+    def z_across(k, r, g=every):
+        return remote(snd2.at[k, g], recv2.at[k, g], snd_sem.at[1], r, emb=across)
 
     def g_at(x, k, rows, count=None):
         return gall.at[x * NK + k if count is None else pl.ds(x * NK + k, count), rows]
@@ -185,43 +186,40 @@
         x = jnp.dot(ohx[k // 2, part_k, :], bother[...], preferred_element_type=F32)
         xbuf[k % 2, 1] = x.astype(BF)
 
-    gather_own(0)
-
-    c_copy().wait_recv()
-    slots(cx_ref, posx_ref)
-
-    def buildx(b, carry):
-        at = pl.multiple_of(dp * NK * EB + b * 2 * EB, 2 * EB)
-        ohx[b] = hot_rows(posx_ref[pl.ds(at, 2 * EB), :]).astype(BF)
-        return carry
-
-    lax.fori_loop(0, NK // 2, buildx, 0)
-    remote(sq_snd, sq_recv.at[pl.ds(3, 4)], sq_s.at[0], sq_r.at[1], dp=xp).wait_recv()
-    h_copy().wait_recv()
-    bother[...] = normed(hx_ref, sq_recv[3] + sq_recv[4] + sq_recv[5] + sq_recv[6])
-    gather_other(0)
-
-    def products(k):
-        w01_wait(k)
+    def products(k, g=every, act=None):
+        if act is not None:
+            activation_wait(act)
+        if g != 1:
+            w01_wait(k)
         for e in range(EB):
             rows = slice(e * CAP, (e + 1) * CAP)
-            x = jnp.concatenate([xbuf[k % 2, 0, rows, :], xbuf[k % 2, 1, rows, :]], axis=0)
+            if g == every:
+                x = jnp.concatenate([xbuf[k % 2, 0, rows, :], xbuf[k % 2, 1, rows, :]], axis=0)
+            else:
+                x = xbuf[k % 2, g, rows, :]
             z = lax.dot_general(x, w01[k, e], (((1,), (1,)), ((), ())), preferred_element_type=F32).astype(BF)
-            zsend[k, 0, rows, :] = z[0:CAP]
-            zsend[k, 1, rows, :] = z[CAP:]
-        if k + 1 < NK:
+            if g != 1:
+                zsend[k, 0, rows, :] = z[0:CAP]
+            if g != 0:
+                zsend[k, 1, rows, :] = z[-CAP:]
+        if g != 0 and k + 1 < NK:
             gather_own(k + 1)
             gather_other(k + 1)
-        z_pair(k, s1_r.at[k]).start()
-        w2_copy(k).start()
-
-    def stage_b(k):
-        z_pair(k, s1_r.at[k]).wait_recv()
+        if act is not None:
+            activations(act)
+        z_pair(k, s1_r.at[NK if g == 1 else k], g).start()
+        if act is not None:
+            activation_send(act)
+        if g != 0:
+            w2_copy(k).start()
+
+    def stage_b(k, g=every):
+        z_pair(k, s1_r.at[NK if g == 1 else k], g).wait_recv()
         near = pl.ds(pl.multiple_of(row * quarter, quarter), quarter)
         far = pl.ds(pl.multiple_of((1 - row) * quarter, quarter), quarter)
-        snd2[k] = (zsend[k, :, other_rows, :].astype(F32) + recv1[k, :, far, :].astype(F32)).astype(BF)
-        z_across(k, s2_r.at[k]).start()
-        own2[k] = zsend[k, :, own_rows, :].astype(F32) + recv1[k, :, near, :].astype(F32)
+        snd2[k, g] = (zsend[k, g, other_rows, :].astype(F32) + recv1[k, g, far, :].astype(F32)).astype(BF)
+        z_across(k, s2_r.at[NK if g == 1 else k], g).start()
+        own2[k, g] = zsend[k, g, own_rows, :].astype(F32) + recv1[k, g, near, :].astype(F32)
 
     low_lane = lax.broadcasted_iota(jnp.int32, (CAP, 128), 1) < 64
 
@@ -233,20 +231,59 @@
         packed = jnp.where(low_lane, high[0:CAP], pltpu.roll(high[CAP:], 64, 1)).astype(BF)
         return jnp.concatenate([low, packed], axis=0)
 
-    def stage_c(k):
-        n = k // 2 * 2
-        z_across(k, s2_r.at[k]).wait_recv()
+    def activation_wait(k):
+        if k == 0:
+            z_across(0, s2_r.at[0], 0).wait_recv()
+            z_across(0, s2_r.at[NK], 1).wait_recv()
+        else:
+            z_across(k, s2_r.at[k]).wait_recv()
+
+    def activations(k):
         gx[k] = activation(k, 1)
+        gall[dp * NK + k, own_g, :] = activation(k, 0)
+
+    def ga(k, x):
+        return ga_r.at[(k // 2 * 2 if k < NK - 2 else 2 * k - NK + 2) + x]
+
+    def activation_send(k):
         x_copy(6, ha_r.at[k], k, emb=across).start()
         x_copy(5, hs_r.at[k], k).start()
         if k >= DIRECT:
-            x_copy(9, ga_r.at[n + 1], k, emb=corner).start()
-            x_copy(10, ga_r.at[n + 1], k, emb=partner).start()
-        gall[dp * NK + k, own_g, :] = activation(k, 0)
+            x_copy(9, ga(k, 1), k, emb=corner).start()
+            x_copy(10, ga(k, 1), k, emb=partner).start()
         g_copy(2, gy_r.at[k], dp, own_g, k, emb=across).start()
-        g_copy(3, ga_r.at[n], dp, own_g, k, emb=partner).start()
+        g_copy(3, ga(k, 0), dp, own_g, k, emb=partner).start()
         if k >= DIRECT:
-            g_copy(11, ga_r.at[n], dp, own_g, k, emb=corner).start()
+            g_copy(11, ga(k, 0), dp, own_g, k, emb=corner).start()
+
+    def stage_c(k):
+        activation_wait(k)
+        activations(k)
+        activation_send(k)
+
+    def logits_sum():
+        logit_pair().wait_recv()
+        lsnd2[...] = lbuf[mine, :] + lrecv1[mine, :]
+        logit_across().start()
+
+    gather_own(0)
+    products(0, 0)
+    logits_sum()
+
+    c_copy().wait_recv()
+    slots(cx_ref, posx_ref)
+
+    def buildx(b, carry):
+        at = pl.multiple_of(dp * NK * EB + b * 2 * EB, 2 * EB)
+        ohx[b] = hot_rows(posx_ref[pl.ds(at, 2 * EB), :]).astype(BF)
+        return carry
+
+    lax.fori_loop(0, NK // 2, buildx, 0)
+    stage_b(0, 0)
+    remote(sq_snd, sq_recv.at[pl.ds(3, 4)], sq_s, sq_r.at[1], dp=xp).wait_recv()
+    h_copy().wait_recv()
+    bother[...] = normed(hx_ref, functools.reduce(lax.add, [sq_recv[n] for n in range(3, 7)]))
+    gather_other(0)
 
     def from_across(k):
         return g_copy(2, gy_r.at[k], dp, other_g, k, emb=across)
@@ -255,13 +292,12 @@
         return g_copy(5, r, xp, rows, k, dp=xp)
 
     def stage_d(k):
-        n = k // 2 * 2
         from_across(k).wait_recv()
-        g_copy(4, ga_r.at[n], dp, other_g, k, emb=partner).start()
+        g_copy(4, ga(k, 0), dp, other_g, k, emb=partner).start()
         from_x(k, own_g, hs_r.at[k]).wait_recv()
-        g_copy(7, ga_r.at[n + 1], xp, own_g, k, emb=partner).start()
+        g_copy(7, ga(k, 1), xp, own_g, k, emb=partner).start()
         from_x(k, other_g, ha_r.at[k]).wait_recv()
-        g_copy(8, ga_r.at[n + 1], xp, other_g, k, emb=partner).start()
+        g_copy(8, ga(k, 1), xp, other_g, k, emb=partner).start()
 
     hw = width // 2
     both, first, second = slice(0, width), slice(0, hw), slice(hw, width)
@@ -271,24 +307,43 @@
 
     def arrived(n):
         w2_copy(n).wait()
-        for k in (n // 2 * 2, n // 2 * 2 + 1):
-            if k >= DIRECT and n % 2 == 0:
-                from_across(k).wait_recv()
-            if k >= DIRECT and n % 2 == 1:
-                from_x(k, own_g, hs_r.at[k]).wait_recv()
-                from_x(k, other_g, ha_r.at[k]).wait_recv()
         g_copy(3, ga_r.at[n], dp if n % 2 == 0 else xp, theirs, n // 2 * 2, 2, emb=partner).wait_recv()
+
+    def expert_out(b, e, hot, prob, buf, to, cols):
+        q, w = e // 2, e % 2
+        gate = jnp.sum(hot.astype(F32) * prob, axis=1, keepdims=True)
+        low = gall[b, q * QUART + w * CAP:q * QUART + (w + 1) * CAP, :]
+        high = gall[b, q * QUART + 2 * CAP:(q + 1) * QUART, w * 64:(w + 1) * 64]
+        y = jnp.dot(jnp.concatenate([low, high], axis=1), w2buf[b * EB + e, :, cols], preferred_element_type=F32)
+        ubuf[buf % 2, to:to + CAP, cols] = (y.astype(BF).astype(F32) * gate).astype(BF)
 
     def down(n, cols):
         p = pair_no(n)
         probs = pt_ref[pl.ds(pl.multiple_of(p * 2 * EB, 2 * EB), 2 * EB), :]
         for e in range(2 * EB):
-            b, q, w = 2 * p + e // EB, e % EB // 2, e % 2
-            gate = jnp.sum(oht[p, e * CAP:(e + 1) * CAP, :].astype(F32) * probs[e:e + 1, :], axis=1, keepdims=True)
-            low = gall[b, q * QUART + w * CAP:q * QUART + (w + 1) * CAP, :]
-            high = gall[b, q * QUART + 2 * CAP:(q + 1) * QUART, w * 64:(w + 1) * 64]
-            y = jnp.dot(jnp.concatenate([low, high], axis=1), w2buf[2 * EB * p + e, :, cols], preferred_element_type=F32)
-            ubuf[n % 2, e * CAP:(e + 1) * CAP, cols] = (y.astype(BF).astype(F32) * gate).astype(BF)
+            expert_out(2 * p + e // EB, e % EB, oht[p, e * CAP:(e + 1) * CAP, :], probs[e:e + 1, :], n, e * CAP, cols)
+
+    def arrived_last(k):
+        if k >= DIRECT:
+            from_across(k).wait_recv()
+            from_x(k, own_g, hs_r.at[k]).wait_recv()
+            from_x(k, other_g, ha_r.at[k]).wait_recv()
+        for x, half_no in ((0, dp), (1, xp)):
+            g_copy(3, ga(k, x), half_no, theirs, k, emb=partner).wait_recv()
+
+    def down_last(k, cols):
+        for x, half_no in ((0, dp), (1, xp)):
+            p = half_no * (NK // 2) + k // 2
+            probs = pt_ref[pl.ds(pl.multiple_of((half_no * NK + k) * EB, EB), EB), :]
+            for e in range(EB):
+                at = (k % 2 * EB + e) * CAP
+                expert_out(half_no * NK + k, e, oht[p, at:at + CAP, :], probs[e:e + 1, :], k, (x * EB + e) * CAP, cols)
+
+    def combine_last(k, cols):
+        part_k = slice(k % 2 * rows_k, (k % 2 + 1) * rows_k)
+        for x, half_no in ((0, dp), (1, xp)):
+            hot = oh[half_no * (NK // 2) + k // 2, :, part_k]
+            macc[:, cols] += jnp.dot(hot, ubuf[k % 2, x * rows_k:(x + 1) * rows_k, cols], preferred_element_type=F32)
 
     def down_both(n):
         arrived(n)
@@ -296,11 +351,6 @@
             combine(n - 1, both)
         down(n, both)
 
-    def logits_sum():
-        logit_pair().wait_recv()
-        lsnd2[...] = lbuf[mine, :] + lrecv1[mine, :]
-        logit_across().start()
-
     def probabilities():
         logit_across().wait_recv()
         logits = lsnd2[...] + lrecv2[...]
@@ -311,47 +361,48 @@
         prob_pair().wait_recv()
         pt_ref[...] = jnp.transpose(pbuf[...])
 
-    products(0)
+    products(0, 1)
     products(1)
-    stage_b(0)
+    stage_b(0, 1)
     products(2)
     stage_b(1)
-    logits_sum()
     products(3)
     stage_b(2)
-    stage_c(0)
-    products(4)
+    products(4, act=0)
     stage_b(3)
-    stage_c(1)
     probabilities()
-    products(5)
+    products(5, act=1)
     stage_b(4)
-    stage_c(2)
-    stage_d(0)
-    products(6)
+    products(6, act=2)
     stage_b(5)
-    stage_c(3)
-    stage_d(1)
     gates()
     products(7)
     stage_b(6)
+    stage_d(0)
+    stage_c(3)
+    stage_b(7)
     stage_c(4)
+    stage_d(1)
+    stage_c(5)
+    down_both(0)
     stage_d(2)
-    down_both(0)
-    stage_b(7)
-    stage_c(5)
+    stage_c(6)
+    down_both(1)
     stage_d(3)
-    down_both(1)
+    stage_c(7)
     stage_d(4)
-    stage_c(6)
     down_both(2)
-    stage_c(7)
     stage_d(5)
     down_both(3)
+    stage_d(6)
     down_both(4)
-    stage_d(6)
     down_both(5)
-    down_both(6)
+    combine(5, both)
+    w2_copy(6).wait()
+    w2_copy(7).wait()
+    arrived_last(6)
+    down_last(6, both)
+    combine_last(6, both)
 
     part = tok // 4
 
@@ -359,16 +410,15 @@
         peer = (ffn + d) % 4
         cols = pl.ds(col * hw, hw)
         return remote(macc.at[pl.ds(pl.multiple_of(peer * part, part), part), cols], mrecv.at[d - 1, :, cols],
-                      rs_s.at[0], rs_r.at[col], ffn=peer)
-
-    arrived(7)
-    combine(6, both)
-    down(7, first)
-    combine(7, first)
+                      rs_s, rs_r.at[col], ffn=peer)
+
+    arrived_last(7)
+    down_last(7, first)
+    combine_last(7, first)
     for d in (2, 1, 3):
         rs_copy(d, 0).start()
-    down(7, second)
-    combine(7, second)
+    down_last(7, second)
+    combine_last(7, second)
     for d in (2, 1, 3):
         rs_copy(d, 1).start()
 
@@ -382,27 +432,27 @@
         x_copy(sem, gy_r.at[0], k, count).wait_send()
     h_copy().wait_send()
     c_copy().wait_send()
-    remote(sq_recv, sq_recv, sq_s.at[0], sq_r.at[0], dp=xp).wait_send()
+    remote(sq_recv, sq_recv, sq_s, sq_r.at[0], dp=xp).wait_send()
     logit_pair().wait_send()
     logit_across().wait_send()
     prob_pair().wait_send()
     m = macc[my_tok, :]
     for col in range(2):
         all_in = mrecv.at[:, :, pl.ds(col * hw, hw)]
-        remote(all_in, all_in, rs_s.at[0], rs_r.at[col], ffn=(ffn + 1) % 4).wait_recv()
+        remote(all_in, all_in, rs_s, rs_r.at[col], ffn=(ffn + 1) % 4).wait_recv()
     for d in range(1, 4):
         m = m + mrecv[d - 1]
     mown[...] = m
     m2 = m * m
-    tq_snd[...] = m2[:, 0:128] + m2[:, 128:256] + m2[:, 256:384] + m2[:, 384:512]
+    tq_snd[...] = functools.reduce(lax.add, jnp.split(m2, width // LANES, axis=1))
 
     def tq_copy(d):
-        return remote(tq_snd, tq_recv.at[d - 1], tq_s.at[0], tq_r.at[0], emb=(emb + d) % 4)
+        return remote(tq_snd, tq_recv.at[d - 1], tq_s, tq_r, emb=(emb + d) % 4)
 
     for d in (2, 3, 1):
         tq_copy(d).start()
-    remote(mrecv, mrecv, rs_s.at[0], rs_r.at[0], ffn=(ffn + 1) % 4).wait_send()
-    remote(tq_recv, tq_recv, tq_s.at[0], tq_r.at[0], emb=partner).wait()
+    remote(mrecv, mrecv, rs_s, rs_r.at[0], ffn=(ffn + 1) % 4).wait_send()
+    remote(tq_recv, tq_recv, tq_s, tq_r, emb=partner).wait()
     tot = tq_snd[...]
     for d in range(1, 4):
         tot = tot + tq_recv[d - 1]
@@ -411,7 +461,7 @@
     obuf[...] = res.astype(BF)
 
     def ag_copy(d):
-        return remote(obuf, o_ref.at[my_tok], ag_s.at[0], ag_r.at[0], ffn=(ffn + d) % 4)
+        return remote(obuf, o_ref.at[my_tok], ag_s, ag_r, ffn=(ffn + d) % 4)
 
     for d in (2, 1, 3):
         ag_copy(d).start()
@@ -419,7 +469,7 @@
     keep.start()
     others = o_ref.at[pl.ds(0, 3 * part)]
     keep.wait()
-    remote(others, others, ag_s.at[0], ag_r.at[0], ffn=(ffn + 1) % 4).wait()
+    remote(others, others, ag_s, ag_r, ffn=(ffn + 1) % 4).wait()
 
 
 def solution(mesh):
@@ -428,7 +478,7 @@
     def local_block(hidden, norm_pre, norm_post, w_router, w_gate, w_up, w_down, choice):
         tok, width = hidden.shape
         experts, _, fw = w_gate.shape
-        dma = pltpu.SemaphoreType.DMA
+        dma = one = pltpu.SemaphoreType.DMA
         vm = pltpu.VMEM
         rows = EB * CAP
         return pl.pallas_call(
@@ -451,9 +501,9 @@
                 vm((8, tok), F32), vm((7, 8, tok), F32),
                 vm((tok, width), F32), vm((2, 2 * rows, width), BF), vm((3, tok // 4, width), F32), vm((tok // 4, width), F32),
                 vm((tok // 4, 128), F32), vm((3, tok // 4, 128), F32), vm((tok // 4, width), BF), vm((2, 2, rows, width), BF),
-                dma((5,)), dma((NK,)), dma((12,)), dma((NK,)), dma((NK,)), dma((NK,)), dma((NK,)), dma((NK,)), dma((NK,)),
-                dma((3,)), dma((3,)), dma((2,)), dma((2,)), dma((1,)), dma((2,)),
-                dma((1,)), dma((2,)), dma((1,)), dma((1,)), dma((1,)), dma((1,)),
+                dma((5,)), dma((NK,)), dma((12,)), dma((NK + 1,)), dma((NK + 1,)), dma((NK,)), dma((NK,)), dma((NK,)), dma((NK + 2,)),
+                dma((3,)), dma((3,)), dma((2,)), dma((2,)), one, dma((2,)),
+                one, dma((2,)), one, one, one, one,
             ],
             compiler_params=pltpu.CompilerParams(
                 collective_id=0, has_side_effects=True, vmem_limit_bytes=67043328),

time: 50 us -> 49.5 us (0.990)
  Pallas kernels: 48.3 us -> 47.7 us
    pallas_call x1, Pallas kernels: 48.3 us -> 47.7 us  [local_block(): pl.pallas_call(functools.partial(kernel, width * emb_size), out_shape=jax...]
where the time goes in v5:
time: 49.5 us; the launch traced here: 49.3 us
  Pallas kernels  47.7 us (96%)
  local copies, waits for them, and re-layouts  1.57 us (3%)
    pallas_call x1, Pallas kernels, local_block(): pl.pallas_call(functools.partial(kernel, width * emb_size), out_shape=jax...  47.7 us
    unnamed x1, local copies, waits for them, and re-layouts  1.57 us

profile of v5, /device:TPU:0, one launch (start us, length us, event | category | flops | bytes accessed | tf_op | source)
XLA Modules:
  0.0 49.3 jit_solution(6511273538822614764)
XLA Ops:
  0.0 47.7 %shard_map.82 = bf16[128,512]{1,0:T(8,128)(2,1)} custom-call(bf16[128,512]{1,0:T(8,128)(2,1)} %h_hbm.1, bf16[512]{0:T(512)(128)(2,1)} %pre_hbm.1, bf16[512]{0:T(512)(128)(2,1)} %post_hbm.1, bf16[512,128]{1,0:T(8,128)(2,1)} %wr_hbm.1, s32[8,128]{1,0:T(8,128)} %bitcast.5, bf16[128,192,512]{2,1,0:T(8,128)(2,1)} %bitcast.3, bf16[128,192,512]{2,1,0:T(8,128)(2,1)} %bitcast.4, ...), custom_call_target="tpu_custom_call" | custom-call | tf_op jit(solution)/shard_map/pallas_call | solution.py:484
  47.7 1.6 %copy.10 = bf16[128,512]{1,0:T(8,128)(2,1)} copy(bf16[128,512]{1,0:T(8,128)(2,1)} %shard_map.82) | data formatting | bytes 262144

commit v6 on v5

--- a/solution.py
+++ b/solution.py
@@ -436,15 +436,14 @@
     logit_pair().wait_send()
     logit_across().wait_send()
     prob_pair().wait_send()
-    m = macc[my_tok, :]
-    for col in range(2):
+    squares = []
+    for col, cols in enumerate((first, second)):
         all_in = mrecv.at[:, :, pl.ds(col * hw, hw)]
         remote(all_in, all_in, rs_s, rs_r.at[col], ffn=(ffn + 1) % 4).wait_recv()
-    for d in range(1, 4):
-        m = m + mrecv[d - 1]
-    mown[...] = m
-    m2 = m * m
-    tq_snd[...] = functools.reduce(lax.add, jnp.split(m2, width // LANES, axis=1))
+        m = functools.reduce(lax.add, [mrecv[d, :, cols] for d in range(3)], macc[my_tok, cols])
+        mown[:, cols] = m
+        squares += jnp.split(m * m, hw // LANES, axis=1)
+    tq_snd[...] = functools.reduce(lax.add, squares)
 
     def tq_copy(d):
         return remote(tq_snd, tq_recv.at[d - 1], tq_s, tq_r, emb=(emb + d) % 4)

time: 49.5 us -> 49.5 us (level)
  no operation moved by 1% of the time
where the time goes in v6:
time: 49.5 us; the launch traced here: 49.3 us
  Pallas kernels  47.7 us (96%)
  local copies, waits for them, and re-layouts  1.57 us (3%)
    pallas_call x1, Pallas kernels, local_block(): pl.pallas_call(functools.partial(kernel, width * emb_size), out_shape=jax...  47.7 us
    unnamed x1, local copies, waits for them, and re-layouts  1.57 us

profile of v6, /device:TPU:0, one launch (start us, length us, event | category | flops | bytes accessed | tf_op | source)
XLA Modules:
  0.0 49.3 jit_solution(5678426162594140905)
XLA Ops:
  0.0 47.7 %shard_map.82 = bf16[128,512]{1,0:T(8,128)(2,1)} custom-call(bf16[128,512]{1,0:T(8,128)(2,1)} %h_hbm.1, bf16[512]{0:T(512)(128)(2,1)} %pre_hbm.1, bf16[512]{0:T(512)(128)(2,1)} %post_hbm.1, bf16[512,128]{1,0:T(8,128)(2,1)} %wr_hbm.1, s32[8,128]{1,0:T(8,128)} %bitcast.5, bf16[128,192,512]{2,1,0:T(8,128)(2,1)} %bitcast.3, bf16[128,192,512]{2,1,0:T(8,128)(2,1)} %bitcast.4, ...), custom_call_target="tpu_custom_call" | custom-call | tf_op jit(solution)/shard_map/pallas_call | solution.py:483
  47.7 1.6 %copy.10 = bf16[128,512]{1,0:T(8,128)(2,1)} copy(bf16[128,512]{1,0:T(8,128)(2,1)} %shard_map.82) | data formatting | bytes 262144
